TPU v7x, 32 devices: a whole 2x2x4 slice. The times are simulated.
32 devices in a mesh: seq: 8 (over y, x, core), kvh: 4 (over z).
Axes of the slice: x: 2, y: 2, z: 4, core: 2. Of those that a mesh axis runs over, the one named last changes fastest.
Arguments:
- hidden: bfloat16 [6144, 4096], P('seq'), may hold values from -32 to 32
- w_query: bfloat16 [4096, 4096], P(None, 'kvh'), may hold values from -0.09375 to 0.09375
- w_key: bfloat16 [4096, 1024], P(None, 'kvh'), may hold values from -0.09375 to 0.09375
- w_value: bfloat16 [4096, 1024], P(None, 'kvh'), may hold values from -0.09375 to 0.09375
- cached_key: bfloat16 [6144, 1024], P('seq', 'kvh'), may hold values from -6 to 6
- cached_value: bfloat16 [6144, 1024], P('seq', 'kvh'), may hold values from -6 to 6
- doc_lengths: int32 [4], replicated, may hold values from 1 to 3072, 6144 in all
- selected: int32 [960], replicated, may hold values from 0 to 767, as said below
Outputs:
- attended: bfloat16 [960, 4096], P('seq', 'kvh')
- score: float32 [6144], P('seq')
Inputs may be any that keep to these rules, and one draw needn't show every extreme that they name: `selected`: each block of 120 entries holds distinct local row numbers in increasing order.
All inputs are finite; a program needn't handle non-finite values.
Results may differ from a plain program's by a relative error of at most 0.02.
Values may be sent and summed in bfloat16 or wider, within the bound.
A program may use at most 192 MiB of HBM per device.

v0:
```python
import functools
import math

import jax
import jax.numpy as jnp
from jax import lax
from jax.experimental import pallas as pl
from jax.experimental.pallas import tpu as pltpu
from jax.sharding import PartitionSpec as P

HEADS = 32
KV_HEADS = 8
HEAD_DIM = 128
GROUP = HEADS // KV_HEADS
EXP_SCALE = HEAD_DIM ** (-0.5) * math.log2(math.e)
MESH = pl.DeviceIdType.MESH
NT = (((1,), (1,)), ((), ()))


def round_up(a, b):
    return -(-a // b) * b


def split_chips(chips):
    small = max(a for a in range(1, math.isqrt(chips) + 1) if chips % a == 0)
    return small, chips // small


def kernel(
    n, kz, docs, sel_rows,
    hid_hbm, wq_hbm, wk_hbm, wv_hbm, ck_hbm, cv_hbm, lens_ref, sel_ref,
    out_ref, score_ref,
    hid, wq, wk, wv, ck, cv, kbuf, vbuf, fresh, hq, q_ref, m_ref, l_ref, acc_ref, dev_ref, bias_ref,
    devbuf, docbuf,
    load_sem, own_send, fwd_send, relay_send, z_send, doc_send, recv, z_recv, doc_recv,
):
    tok = hid.shape[0]
    width = hid.shape[1]
    cols = wk.shape[1]
    local_heads = cols // HEAD_DIM
    pad = round_up(sel_rows, 16)
    qrows = GROUP * pad
    plain = tok - sel_rows
    cut = plain // 16 * 16
    parts = ((0, cut), (cut, tok - cut))
    bufs = (kbuf, vbuf)
    rows_a, rows_b = split_chips(n // 2)
    me = lax.axis_index("seq")
    zme = lax.axis_index("kvh")
    core = me % 2
    xx = (me // 2) % rows_b
    yy = me // (2 * rows_b)
    partner = me + 1 - 2 * core

    def at(dy, dx, dc=0):
        y = (yy + dy) % rows_a
        x = (xx + dx) % rows_b
        return (y * rows_b + x) * 2 + (core + dc) % 2

    half = tok // 2
    loads = [
        pltpu.make_async_copy(ck_hbm, ck, load_sem.at[0]),
        pltpu.make_async_copy(cv_hbm, cv, load_sem.at[1]),
        pltpu.make_async_copy(wk_hbm, wk, load_sem.at[2]),
        pltpu.make_async_copy(hid_hbm.at[pl.ds(0, half)], hid.at[pl.ds(0, half)], load_sem.at[3]),
        pltpu.make_async_copy(wv_hbm, wv, load_sem.at[4]),
        pltpu.make_async_copy(hid_hbm.at[pl.ds(half, half)], hid.at[pl.ds(half, half)], load_sem.at[5]),
        pltpu.make_async_copy(wq_hbm, wq, load_sem.at[6]),
    ]
    for load in loads:
        load.start()

    barrier = pltpu.get_barrier_semaphore()
    for d in range(1, n):
        pl.semaphore_signal(barrier, inc=1, device_id={"seq": (me + d) % n}, device_id_type=MESH)
    for d in range(1, kz):
        pl.semaphore_signal(barrier, inc=1, device_id={"kvh": (zme + d) % kz}, device_id_type=MESH)

    lane = lax.broadcasted_iota(jnp.int32, (8, tok), 1)

    def mark(r, chosen):
        return jnp.where(lane == sel_ref[me * sel_rows + r], 1, chosen)

    chosen = lax.fori_loop(0, sel_rows, mark, jnp.zeros((8, tok), jnp.int32), unroll=8)
    upper = (
        lax.broadcasted_iota(jnp.int32, (tok, tok), 0)
        <= lax.broadcasted_iota(jnp.int32, (tok, tok), 1)
    ).astype(jnp.float32).astype(jnp.bfloat16)
    count = jnp.dot(
        chosen.astype(jnp.float32).astype(jnp.bfloat16), upper, preferred_element_type=jnp.float32
    ).astype(jnp.int32)
    target = jnp.where(chosen > 0, plain + count - 1, lane - count)[0:1]

    def place(first, rows):
        row = lax.broadcasted_iota(jnp.int32, (rows, tok), 0) + first
        return (row == target).astype(jnp.float32).astype(jnp.bfloat16)

    first_place = place(0, cut)
    loads[0].wait()
    kbuf[me, 0:cut, :] = jnp.dot(first_place, ck[...], preferred_element_type=jnp.float32).astype(
        jnp.bfloat16
    )
    loads[1].wait()
    vbuf[me, 0:cut, :] = jnp.dot(first_place, cv[...], preferred_element_type=jnp.float32).astype(
        jnp.bfloat16
    )
    pl.semaphore_wait(barrier, n - 1 + kz - 1)

    def remote(src, arr, part, send_sem, dest):
        view = bufs[arr].at[src, pl.ds(parts[part][0], parts[part][1])]
        return pltpu.make_async_remote_copy(
            src_ref=view, dst_ref=view, send_sem=send_sem, recv_sem=recv.at[src, arr, part],
            device_id={"seq": dest}, device_id_type=MESH,
        )

    sends = []

    def relay(src, s, part):
        for arr in (0, 1):
            remote(src, arr, part, relay_send.at[s, arr, part], partner).start()

    def send_own(part):
        relay(me, 0, part)
        for order in (0, 1):
            for d in range(1, rows_b):
                sends.append(remote(me, order, part, own_send.at[order, part, d - 1], at(0, d)))
                sends[-1].start()
            for d in range(1, rows_a):
                arr = 1 - order
                sends.append(
                    remote(me, arr, part, own_send.at[arr, part, rows_b - 1 + d - 1], at(d, 0))
                )
                sends[-1].start()

    def forward(part):
        for dx in range(1, rows_b):
            src = at(0, dx)
            remote(src, 0, part, own_send.at[0, part, 0], partner).wait_recv()
            for dy in range(1, rows_a):
                sem = fwd_send.at[0, part, (dx - 1) * (rows_a - 1) + dy - 1]
                sends.append(remote(src, 0, part, sem, at(dy, 0)))
                sends[-1].start()
        for dy in range(1, rows_a):
            src = at(dy, 0)
            remote(src, 1, part, own_send.at[0, part, 0], partner).wait_recv()
            for dx in range(1, rows_b):
                sem = fwd_send.at[1, part, (dx - 1) * (rows_a - 1) + dy - 1]
                sends.append(remote(src, 1, part, sem, at(0, dx)))
                sends[-1].start()

    send_own(0)

    loads[2].wait()
    for piece in range(2):
        rows = pl.ds(piece * half, half)
        loads[3 + 2 * piece].wait()
        key_fresh = jnp.dot(hid[rows, :], wk[...], preferred_element_type=jnp.float32)
        fresh[0, rows, :] = key_fresh.astype(jnp.bfloat16)
        key_shift = key_fresh - ck[rows, :].astype(jnp.float32)
        square = key_shift * key_shift
        if piece == 0:
            loads[4].wait()
        value_fresh = jnp.dot(hid[rows, :], wv[...], preferred_element_type=jnp.float32)
        fresh[1, rows, :] = value_fresh.astype(jnp.bfloat16)
        value_shift = value_fresh - cv[rows, :].astype(jnp.float32)
        square = square + value_shift * value_shift
        folded = square[:, 0:HEAD_DIM]
        for h in range(1, local_heads):
            folded = folded + square[:, h * HEAD_DIM:(h + 1) * HEAD_DIM]
        total = jnp.sum(folded.T, axis=0, keepdims=True)
        dev_ref[:, piece * half:(piece + 1) * half] = jnp.broadcast_to(total, (8, half))

    last_row = lax.broadcasted_iota(jnp.int32, (tok - cut, tok), 0) + cut
    hit = last_row == target
    old = jnp.where(hit & (last_row < plain), 1.0, 0.0).astype(jnp.bfloat16)
    new = jnp.where(hit & (last_row >= plain), 1.0, 0.0).astype(jnp.bfloat16)
    for arr, cached in enumerate((ck, cv)):
        tail = jnp.dot(old, cached[...], preferred_element_type=jnp.float32)
        tail = tail + jnp.dot(new, fresh[arr], preferred_element_type=jnp.float32)
        bufs[arr][me, cut:tok, :] = tail.astype(jnp.bfloat16)
    devbuf[zme] = dev_ref[...]
    send_own(1)
    forward(0)
    for d in range(1, kz):
        sends.append(
            pltpu.make_async_remote_copy(
                src_ref=devbuf.at[zme], dst_ref=devbuf.at[zme], send_sem=z_send.at[d - 1],
                recv_sem=z_recv.at[zme], device_id={"kvh": (zme + d) % kz}, device_id_type=MESH,
            )
        )
        sends[-1].start()

    pick = place(plain, pad)
    step = width // 4
    for c in range(4):
        chunk = slice(c * step, (c + 1) * step)
        hq[:, chunk] = jnp.dot(pick, hid[:, chunk], preferred_element_type=jnp.float32).astype(
            jnp.bfloat16
        )
    loads[6].wait()

    def project(h, carry):
        chunk = pl.ds(pl.multiple_of(h * GROUP * HEAD_DIM, HEAD_DIM), GROUP * HEAD_DIM)
        queries = jnp.dot(hq[...], wq[:, chunk], preferred_element_type=jnp.float32).astype(
            jnp.bfloat16
        )
        for g in range(GROUP):
            q_ref[h, g * pad:(g + 1) * pad, :] = queries[:, g * HEAD_DIM:(g + 1) * HEAD_DIM]
        return carry

    lax.fori_loop(0, local_heads, project, 0)

    code = jnp.where(
        lax.broadcasted_iota(jnp.int32, (8, tok), 0) == 0, lane % 256, lane // 256
    ).astype(jnp.float32).astype(jnp.bfloat16)
    found = lax.dot_general(code, place(0, tok), NT, preferred_element_type=jnp.float32)
    key_pos = (found[0:1] + 256.0 * found[1:2]).astype(jnp.int32)
    pad_lane = lax.broadcasted_iota(jnp.int32, (pad, tok), 1)
    row_pos = jnp.sum(
        jnp.where(pick.astype(jnp.float32) > 0, pad_lane.astype(jnp.float32), 0.0),
        axis=1, keepdims=True,
    ).astype(jnp.int32)
    bias_ref[...] = jnp.where(key_pos <= row_pos, 0.0, -1e30)

    chunks = 1
    crows = qrows // chunks

    def attend(src, h, c, keys, own):
        rows = slice(c * crows, (c + 1) * crows)
        head = slice(h * HEAD_DIM, (h + 1) * HEAD_DIM)
        scores = lax.dot_general(
            q_ref[h, rows, :], kbuf[src, keys, head], NT, preferred_element_type=jnp.float32
        )
        if own:
            scores = scores + jnp.concatenate([bias_ref[...]] * (crows // pad), axis=0)
        best = jnp.max(scores, axis=1, keepdims=True)
        if not own:
            before = m_ref[h, rows, :]
            best = jnp.maximum(best, before)
        weights = jnp.exp2((scores - best) * EXP_SCALE)
        row_sum = jnp.sum(weights, axis=1, keepdims=True)
        mixed = jnp.dot(
            weights.astype(jnp.bfloat16), vbuf[src, keys, head], preferred_element_type=jnp.float32
        )
        if not own:
            fade = jnp.exp2((before - best) * EXP_SCALE)
            row_sum = row_sum + l_ref[h, rows, :] * fade
            mixed = mixed + acc_ref[h, rows, :] * fade
        m_ref[h, rows, :] = best
        l_ref[h, rows, :] = row_sum
        acc_ref[h, rows, :] = mixed

    def attend_all(src, first, count, own):
        for h in range(local_heads):
            for c in range(chunks):
                attend(src, h, c, slice(first, first + count), own)

    attend_all(me, 0, tok, True)

    for d in range(1, kz):
        src = (zme + d) % kz
        pltpu.make_async_remote_copy(
            src_ref=devbuf.at[src], dst_ref=devbuf.at[src], send_sem=z_send.at[0],
            recv_sem=z_recv.at[src], device_id={"kvh": src}, device_id_type=MESH,
        ).wait_recv()
    deviation = devbuf[0]
    for z in range(1, kz):
        deviation = deviation + devbuf[z]
    deviation = deviation[0:1]
    position = lane[0:1] + me * tok
    inside = []
    end = jnp.int32(0)
    for d in range(docs):
        begin, end = end, end + lens_ref[d]
        inside.append((position >= begin) & (position < end))
    slot_row = lax.broadcasted_iota(jnp.int32, docbuf.shape[1:], 0)
    shares = jnp.zeros(docbuf.shape[1:], jnp.float32)
    for d in range(docs):
        share = jnp.sum(jnp.where(inside[d], deviation, 0.0), axis=1, keepdims=True)
        shares = jnp.where(slot_row == d, share, shares)
    docbuf[me] = shares
    for d in range(1, n):
        sends.append(
            pltpu.make_async_remote_copy(
                src_ref=docbuf.at[me], dst_ref=docbuf.at[me], send_sem=doc_send.at[d - 1],
                recv_sem=doc_recv.at[me], device_id={"seq": (me + d) % n}, device_id_type=MESH,
            )
        )
        sends[-1].start()

    def other(part, s, carry):
        dc = s % 2
        dx = (s // 2) % rows_b
        dy = s // (2 * rows_b)
        src = at(dy, dx, dc)
        idle = own_send.at[0, part, 0]

        @pl.when((dc == 1) | (dy != 0))
        def _():
            remote(src, 0, part, idle, partner).wait_recv()

        @pl.when((dc == 1) | (dx != 0))
        def _():
            remote(src, 1, part, idle, partner).wait_recv()

        @pl.when(dc == 0)
        def _():
            relay(src, s // 2, part)

        @pl.when(src < me)
        def _():
            attend_all(src, *parts[part], False)

        return carry

    lax.fori_loop(1, n - 2, functools.partial(other, 0), 0)
    forward(1)
    lax.fori_loop(n - 2, n, functools.partial(other, 0), 0)
    lax.fori_loop(1, n, functools.partial(other, 1), 0)

    for h in range(local_heads):
        done = (acc_ref[h] / l_ref[h]).astype(jnp.bfloat16)
        for g in range(GROUP):
            head = h * GROUP + g
            out_ref[:, head * HEAD_DIM:(head + 1) * HEAD_DIM] = done[g * pad:g * pad + sel_rows]

    for d in range(1, n):
        src = (me + d) % n
        pltpu.make_async_remote_copy(
            src_ref=docbuf.at[src], dst_ref=docbuf.at[src], send_sem=doc_send.at[0],
            recv_sem=doc_recv.at[src], device_id={"seq": src}, device_id_type=MESH,
        ).wait_recv()
    totals = docbuf[0]
    for s in range(1, n):
        totals = totals + docbuf[s]
    mean = jnp.zeros((1, tok), jnp.float32)
    for d in range(docs):
        here = totals[d:d + 1, 0:1] / lens_ref[d].astype(jnp.float32)
        mean = jnp.where(inside[d], here, mean)
    score_ref[...] = deviation / (mean + 1.0)

    for send in sends:
        send.wait_send()

    def drain(s, carry):
        for part in (0, 1):
            for arr in (0, 1):
                remote(me, arr, part, relay_send.at[s, arr, part], partner).wait_send()
        return carry

    lax.fori_loop(0, n // 2, drain, 0)


def shards(n, kz, hidden, w_query, w_key, w_value, cached_key, cached_value, doc_lengths, selected):
    tok, width = hidden.shape
    cols = w_key.shape[1]
    qcols = w_query.shape[1]
    sel_rows = selected.shape[0] // n
    docs = doc_lengths.shape[0]
    pad = round_up(sel_rows, 16)
    local_heads = cols // HEAD_DIM
    qrows = GROUP * pad
    rows_a, rows_b = split_chips(n // 2)
    peers = max(1, rows_a + rows_b - 2)
    forwards = max(1, (rows_a - 1) * (rows_b - 1))
    bf, f32 = jnp.bfloat16, jnp.float32
    dma = pltpu.SemaphoreType.DMA
    any_space = pl.BlockSpec(memory_space=pl.ANY)
    vmem = pl.BlockSpec(memory_space=pltpu.VMEM)
    smem = pl.BlockSpec(memory_space=pltpu.SMEM)
    attended, score = pl.pallas_call(
        functools.partial(kernel, n, kz, docs, sel_rows),
        out_shape=(
            jax.ShapeDtypeStruct((sel_rows, qcols), bf),
            jax.ShapeDtypeStruct((1, tok), f32),
        ),
        in_specs=[any_space] * 6 + [smem] * 2,
        out_specs=(vmem, vmem),
        scratch_shapes=[
            pltpu.VMEM((tok, width), bf),
            pltpu.VMEM((width, qcols), bf),
            pltpu.VMEM((width, cols), bf),
            pltpu.VMEM((width, cols), bf),
            pltpu.VMEM((tok, cols), bf),
            pltpu.VMEM((tok, cols), bf),
            pltpu.VMEM((n, tok, cols), bf),
            pltpu.VMEM((n, tok, cols), bf),
            pltpu.VMEM((2, tok, cols), bf),
            pltpu.VMEM((pad, width), bf),
            pltpu.VMEM((local_heads, qrows, HEAD_DIM), bf),
            pltpu.VMEM((local_heads, qrows, 1), f32),
            pltpu.VMEM((local_heads, qrows, 1), f32),
            pltpu.VMEM((local_heads, qrows, HEAD_DIM), f32),
            pltpu.VMEM((8, tok), f32),
            pltpu.VMEM((pad, tok), f32),
            pltpu.VMEM((kz, 8, tok), f32),
            pltpu.VMEM((n, round_up(docs, 8), 128), f32),
            dma((7,)),
            dma((2, 2, peers)),
            dma((2, 2, forwards)),
            dma((n // 2, 2, 2)),
            dma((max(1, kz - 1),)),
            dma((n - 1,)),
            dma((n, 2, 2)),
            dma((kz,)),
            dma((n,)),
        ],
        compiler_params=pltpu.CompilerParams(
            collective_id=0, has_side_effects=True, vmem_limit_bytes=62 * 1024 * 1024
        ),
        name="blend",
    )(hidden, w_query, w_key, w_value, cached_key, cached_value, doc_lengths, selected)
    return attended, score.reshape(tok)


def solution(mesh):
    return jax.shard_map(
        functools.partial(shards, mesh.shape["seq"], mesh.shape["kvh"]),
        mesh=mesh,
        in_specs=(
            P("seq", None),
            P(None, "kvh"),
            P(None, "kvh"),
            P(None, "kvh"),
            P("seq", "kvh"),
            P("seq", "kvh"),
            P(),
            P(),
        ),
        out_specs=(P("seq", "kvh"), P("seq")),
        check_vma=False,
    )
```

profile of v0, /device:TPU:7, one launch (start us, length us, event | category | flops | bytes accessed | tf_op | source)
XLA Modules:
  0.0 46.7 jit_solution(13169180267332611419)
XLA Ops:
  0.6 43.1 %blend.1 = (bf16[120,1024]{1,0:T(8,128)(2,1)}, f32[1,768]{1,0:T(1,128)}) custom-call(bf16[768,4096]{1,0:T(8,128)(2,1)} %hid_hbm.1, bf16[4096,1024]{1,0:T(8,128)(2,1)} %wq_hbm.1, bf16[4096,256]{1,0:T(8,128)(2,1)} %wk_hbm.1, bf16[4096,256]{1,0:T(8,128)(2,1)} %wv_hbm.1, bf16[768,256]{1,0:T(8,128)(2,1)} %ck_hbm.1, bf16[768,256]{1,0:T(8,128)(2,1)} %cv_hbm.1, ...), custom_call_target="tpu_custom_call" | custom-call | tf_op jit(solution)/shard_map/blend/pallas_call | solution.py:371
  43.8 1.3 %reduce = f32[768]{0:T(1024)} reduce(f32[1,768]{1,0:T(1,128)} %get-tuple-element.5, f32[]{:T(128)} %constant), dimensions={0}, to_apply=%get-tuple-element.5.reduce_sub_computation | reduce | bytes 6148 | tf_op jit(solution)/shard_map/blend/pallas_call | solution.py:371
  45.0 1.7 %copy.11 = bf16[120,1024]{1,0:T(8,128)(2,1)} copy(bf16[120,1024]{1,0:T(8,128)(2,1)} %get-tuple-element.8) | data formatting | bytes 491520
where the time goes:
time: 46.9 us; the launch traced here: 46.7 us
  Pallas kernels  43.1 us (92%)
  local copies, waits for them, and re-layouts  1.65 us (4%)
  other arithmetic  1.29 us (3%)
  between operations  0.64 us (1%)
    pallas_call x1, Pallas kernels, shards(): pl.pallas_call(functools.partial(kernel, n, kz, docs, sel_rows), out_shap...  43.1 us
    unnamed x1, local copies, waits for them, and re-layouts  1.65 us
    pallas_call x1, other arithmetic, shards(): pl.pallas_call(functools.partial(kernel, n, kz, docs, sel_rows), out_shap...  1.29 us

commit v1 on v0

v1 whole, which is shorter than its diff:
```python
import functools
import math

import jax
import jax.numpy as jnp
from jax import lax
from jax.experimental import pallas as pl
from jax.experimental.pallas import tpu as pltpu
from jax.sharding import PartitionSpec as P

HEADS = 32
KV_HEADS = 8
HEAD_DIM = 128
GROUP = HEADS // KV_HEADS
EXP_SCALE = HEAD_DIM ** (-0.5) * math.log2(math.e)
MESH = pl.DeviceIdType.MESH
NT = (((1,), (1,)), ((), ()))
LANES = 128
EXTRA = 16
HID_CHUNKS = 4


def round_up(a, b):
    return -(-a // b) * b


def kernel(
    n, kz, docs, sel_rows,
    hid_hbm, wq_hbm, wk_hbm, wv_hbm, ck_hbm, cv_hbm, lens_ref, sel_ref,
    out_ref, score_ref,
    hid, wq, wk, wv, ck, cv, hq, kbuf, vbuf, qbuf, pout, pout_stat, pin, pin_stat,
    m_ref, acc_ref, bias_ref, chosen_ref, dev_ref, devbuf, docbuf,
    load_sem, q_send, q_recv, p_send, p_recv, kv_send, kv_recv, z_send, z_recv, doc_send, doc_recv,
):
    tok, width = hid.shape
    heads = wk.shape[1] // HEAD_DIM
    pad = hq.shape[0]
    qrows = GROUP * pad
    qcols = GROUP * HEAD_DIM
    chips = n // 2
    me = lax.axis_index("seq")
    zme = lax.axis_index("kvh")
    core = me % 2
    chip = me // 2
    partner = me + 1 - 2 * core
    step = width // HID_CHUNKS

    def load(src, dst, sem):
        copy = pltpu.make_async_copy(src, dst, load_sem.at[sem])
        copy.start()
        return copy

    hid_loads, wq_loads = [], []
    for c in range(HID_CHUNKS):
        part = pl.ds(c * step, step)
        hid_loads.append(load(hid_hbm.at[:, part], hid.at[:, part], c))
        wq_loads.append(
            load(
                wq_hbm.at[part, pl.ds(0, qcols)], wq.at[part, pl.ds(0, qcols)], HID_CHUNKS + c
            )
        )
    base = 2 * HID_CHUNKS
    ck_load = load(ck_hbm, ck, base)
    rest_loads = [
        load(
            wq_hbm.at[:, pl.ds(h * qcols, qcols)], wq.at[:, pl.ds(h * qcols, qcols)], base + 3 + h
        )
        for h in range(1, heads)
    ]
    wk_load = load(wk_hbm, wk, base + 1)
    cv_load = load(cv_hbm, cv, base + 2)
    wv_load = load(wv_hbm, wv, base + 3)

    barrier = pltpu.get_barrier_semaphore()
    for d in range(1, n):
        pl.semaphore_signal(barrier, inc=1, device_id={"seq": (me + d) % n}, device_id_type=MESH)
    for d in range(1, kz):
        pl.semaphore_signal(barrier, inc=1, device_id={"kvh": (zme + d) % kz}, device_id_type=MESH)

    slot = lax.broadcasted_iota(jnp.int32, (8, pad), 1)

    def place(r, row):
        return jnp.where(slot == r, sel_ref[me * sel_rows + r], row)

    row_pos = lax.fori_loop(0, sel_rows, place, jnp.full((8, pad), -1, jnp.int32), unroll=8)[0:1]
    row_col = jnp.broadcast_to(row_pos.astype(jnp.float32), (LANES, pad)).T
    lane = lax.broadcasted_iota(jnp.int32, (pad, LANES), 1).astype(jnp.float32)
    pick = jnp.concatenate(
        [
            jnp.where(row_col == lane + float(k * LANES), 1.0, 0.0).astype(jnp.bfloat16)
            for k in range(tok // LANES)
        ],
        axis=1,
    )
    key_row = lax.broadcasted_iota(jnp.int32, (tok, pad), 0)
    pick_t = jnp.where(key_row == row_pos, 1.0, 0.0).astype(jnp.bfloat16)
    chosen_ref[...] = jnp.dot(
        pick_t, jnp.ones((pad, LANES), jnp.bfloat16), preferred_element_type=jnp.float32
    )
    bias_ref[...] = jnp.where(key_row <= row_pos, 0.0, -1e30)
    for h in range(heads):
        vbuf[core, h, HEAD_DIM:, :] = jnp.ones((EXTRA, tok), jnp.bfloat16)

    def q_copy(src, h, dest):
        view = qbuf.at[src, h]
        return pltpu.make_async_remote_copy(
            src_ref=view, dst_ref=view, send_sem=q_send.at[dest // 2, h],
            recv_sem=q_recv.at[src, h], device_id={"seq": dest}, device_id_type=MESH,
        )

    def send_queries(h, queries):
        scaled = (queries * EXP_SCALE).astype(jnp.bfloat16)
        for g in range(GROUP):
            qbuf[chip, h, g * pad:(g + 1) * pad, :] = scaled[:, g * HEAD_DIM:(g + 1) * HEAD_DIM]

        def send(s, carry):
            q_copy(chip, h, (chip - 1 - s) * 2 + core).start()
            return carry

        lax.fori_loop(0, chip, send, 0)

    queries = jnp.zeros((pad, qcols), jnp.float32)
    for c in range(HID_CHUNKS):
        part = slice(c * step, (c + 1) * step)
        hid_loads[c].wait()
        picked = jnp.dot(pick, hid[:, part], preferred_element_type=jnp.float32)
        picked = picked.astype(jnp.bfloat16)
        hq[:, part] = picked
        wq_loads[c].wait()
        queries = queries + jnp.dot(picked, wq[part, 0:qcols], preferred_element_type=jnp.float32)
    pl.semaphore_wait(barrier, n - 1 + kz - 1)
    send_queries(0, queries)
    for h in range(1, heads):
        rest_loads[h - 1].wait()
        send_queries(
            h,
            jnp.dot(
                hq[...], wq[:, h * qcols:(h + 1) * qcols], preferred_element_type=jnp.float32
            ),
        )

    def kv_copy(arr, which):
        view = (kbuf, vbuf)[arr].at[which]
        return pltpu.make_async_remote_copy(
            src_ref=view, dst_ref=view, send_sem=kv_send.at[arr], recv_sem=kv_recv.at[arr],
            device_id={"seq": partner}, device_id_type=MESH,
        )

    pieces = 2 if tok % (2 * LANES) == 0 else 1
    half = tok // pieces

    def fold(shift):
        square = shift * shift
        folded = square[:, 0:HEAD_DIM]
        for h in range(1, heads):
            folded = folded + square[:, h * HEAD_DIM:(h + 1) * HEAD_DIM]
        return jnp.sum(folded.T, axis=0, keepdims=True)

    ck_load.wait()
    wk_load.wait()
    key_dev = []
    for p in range(pieces):
        rows = slice(p * half, (p + 1) * half)
        fresh = jnp.dot(hid[rows, :], wk[...], preferred_element_type=jnp.float32)
        cached = ck[rows, :].astype(jnp.float32)
        key_dev.append(fold(fresh - cached))
        mask = jnp.concatenate([chosen_ref[rows, :]] * heads, axis=1) > 0.5
        used = jnp.where(mask, fresh, cached).astype(jnp.bfloat16)
        for h in range(heads):
            kbuf[core, h, rows, :] = used[:, h * HEAD_DIM:(h + 1) * HEAD_DIM]
    kv_copy(0, core).start()
    cv_load.wait()
    wv_load.wait()
    for p in range(pieces):
        rows = slice(p * half, (p + 1) * half)
        fresh = jnp.dot(hid[rows, :], wv[...], preferred_element_type=jnp.float32)
        cached = cv[rows, :].astype(jnp.float32)
        total = key_dev[p] + fold(fresh - cached)
        dev_ref[:, rows] = jnp.broadcast_to(total, (8, half))
        mask = jnp.concatenate([chosen_ref[rows, :]] * heads, axis=1) > 0.5
        used = jnp.where(mask, fresh, cached).T.astype(jnp.bfloat16)
        for h in range(heads):
            vbuf[core, h, 0:HEAD_DIM, rows] = used[h * HEAD_DIM:(h + 1) * HEAD_DIM, :]
    kv_copy(1, core).start()
    devbuf[zme] = dev_ref[...]
    sends = []
    for d in range(1, kz):
        sends.append(
            pltpu.make_async_remote_copy(
                src_ref=devbuf.at[zme], dst_ref=devbuf.at[zme], send_sem=z_send.at[d - 1],
                recv_sem=z_recv.at[zme], device_id={"kvh": (zme + d) % kz}, device_id_type=MESH,
            )
        )
        sends[-1].start()

    cols = 2 * LANES if qrows % (2 * LANES) == 0 else LANES
    col_parts = [slice(j, j + cols) for j in range(0, qrows, cols)]

    def run(items):
        def scores_of(item):
            src, h, block, part, masked, _ = item
            s = lax.dot_general(
                kbuf[block, h], qbuf[src, h, part, :], NT, preferred_element_type=jnp.float32
            )
            if masked:
                first = part.start % pad
                if cols <= pad:
                    bias = bias_ref[:, first:first + cols]
                else:
                    bias = jnp.concatenate([bias_ref[...]] * (cols // pad), axis=1)
                s = s + bias
            return s

        scores = scores_of(items[0])
        for i, (src, h, block, part, masked, sink) in enumerate(items):
            following = scores_of(items[i + 1]) if i + 1 < len(items) else None
            best = jnp.max(scores, axis=0, keepdims=True)
            weights = jnp.exp2(scores - best).astype(jnp.bfloat16)
            mixed = jnp.dot(vbuf[block, h], weights, preferred_element_type=jnp.float32)
            sink(best, mixed)
            scores = following

    def merge(a, b):
        best = jnp.maximum(a[0], b[0])
        return best, a[1] * jnp.exp2(a[0] - best) + b[1] * jnp.exp2(b[0] - best)

    def first_sink(h, part):
        def sink(best, mixed):
            m_ref[h, 0:1, part] = best
            acc_ref[h, :, part] = mixed
        return sink

    def more_sink(h, part):
        def sink(best, mixed):
            best, mixed = merge((m_ref[h, 0:1, part], acc_ref[h, :, part]), (best, mixed))
            m_ref[h, 0:1, part] = best
            acc_ref[h, :, part] = mixed
        return sink

    run([(chip, h, core, part, True, first_sink(h, part)) for h in range(heads) for part in col_parts])
    kv_copy(0, 1 - core).wait_recv()
    kv_copy(1, 1 - core).wait_recv()

    @pl.when(core == 1)
    def _():
        run(
            [
                (chip, h, 0, part, False, more_sink(h, part))
                for h in range(heads)
                for part in col_parts
            ]
        )

    for d in range(1, kz):
        src = (zme + d) % kz
        pltpu.make_async_remote_copy(
            src_ref=devbuf.at[src], dst_ref=devbuf.at[src], send_sem=z_send.at[0],
            recv_sem=z_recv.at[src], device_id={"kvh": src}, device_id_type=MESH,
        ).wait_recv()
    deviation = devbuf[0]
    for z in range(1, kz):
        deviation = deviation + devbuf[z]
    deviation = deviation[0:1]
    position = lax.broadcasted_iota(jnp.int32, (1, tok), 1) + me * tok
    inside = []
    end = jnp.int32(0)
    for d in range(docs):
        begin, end = end, end + lens_ref[d]
        inside.append((position >= begin) & (position < end))
    slot_row = lax.broadcasted_iota(jnp.int32, docbuf.shape[1:], 0)
    shares = jnp.zeros(docbuf.shape[1:], jnp.float32)
    for d in range(docs):
        share = jnp.sum(jnp.where(inside[d], deviation, 0.0), axis=1, keepdims=True)
        shares = jnp.where(slot_row == d, share, shares)
    docbuf[me] = shares
    for d in range(1, n):
        sends.append(
            pltpu.make_async_remote_copy(
                src_ref=docbuf.at[me], dst_ref=docbuf.at[me], send_sem=doc_send.at[d - 1],
                recv_sem=doc_recv.at[me], device_id={"seq": (me + d) % n}, device_id_type=MESH,
            )
        )
        sends[-1].start()

    def p_copies(src_chip, h, dest_chip):
        dest = {"seq": dest_chip * 2 + core}
        return [
            pltpu.make_async_remote_copy(
                src_ref=pout.at[dest_chip, h], dst_ref=pin.at[src_chip, h],
                send_sem=p_send.at[dest_chip, h, 0], recv_sem=p_recv.at[src_chip, h, 0],
                device_id=dest, device_id_type=MESH,
            ),
            pltpu.make_async_remote_copy(
                src_ref=pout_stat.at[dest_chip, h], dst_ref=pin_stat.at[src_chip, h],
                send_sem=p_send.at[dest_chip, h, 1], recv_sem=p_recv.at[src_chip, h, 1],
                device_id=dest, device_id_type=MESH,
            ),
        ]

    above = chips - 1 - chip
    stat_row = lax.broadcasted_iota(jnp.int32, (8, cols), 0)

    def serve(i, carry):
        h = i // above
        src = chip + 1 + i % above
        q_copy(src, h, me).wait_recv()
        held = {}

        def keep(part):
            def sink(best, mixed):
                held[part.start] = (best, mixed)
            return sink

        def finish(part):
            def sink(best, mixed):
                best, mixed = merge(held[part.start], (best, mixed))
                pout[src, h, :, part] = mixed[0:HEAD_DIM].astype(jnp.bfloat16)
                pout_stat[src, h, :, part] = jnp.where(
                    stat_row == 0, best, mixed[HEAD_DIM:HEAD_DIM + 8]
                )
            return sink

        items = []
        for part in col_parts:
            items.append((src, h, 0, part, False, keep(part)))
            items.append((src, h, 1, part, False, finish(part)))
        run(items)
        for copy in p_copies(chip, h, src):
            copy.start()
        return carry

    lax.fori_loop(0, heads * above, serve, 0)

    for d in range(1, n):
        src = (me + d) % n
        pltpu.make_async_remote_copy(
            src_ref=docbuf.at[src], dst_ref=docbuf.at[src], send_sem=doc_send.at[0],
            recv_sem=doc_recv.at[src], device_id={"seq": src}, device_id_type=MESH,
        ).wait_recv()
    totals = docbuf[0]
    for s in range(1, n):
        totals = totals + docbuf[s]
    mean = jnp.zeros((1, tok), jnp.float32)
    for d in range(docs):
        here = totals[d:d + 1, 0:1] / lens_ref[d].astype(jnp.float32)
        mean = jnp.where(inside[d], here, mean)
    score_ref[...] = deviation / (mean + 1.0)

    def gather(i, carry):
        src = chip - 1 - i // heads
        h = i % heads
        for copy in p_copies(src, h, chip):
            copy.wait_recv()
        best = m_ref[h, 0:1, :]
        other = pin_stat[src, h, 0:1, :]
        top = jnp.maximum(best, other)
        fade, rise = jnp.exp2(best - top), jnp.exp2(other - top)
        m_ref[h, 0:1, :] = top
        acc_ref[h, 0:HEAD_DIM, :] = (
            acc_ref[h, 0:HEAD_DIM, :] * fade + pin[src, h].astype(jnp.float32) * rise
        )
        acc_ref[h, HEAD_DIM:HEAD_DIM + 1, :] = (
            acc_ref[h, HEAD_DIM:HEAD_DIM + 1, :] * fade + pin_stat[src, h, 1:2, :] * rise
        )
        return carry

    lax.fori_loop(0, chip * heads, gather, 0)

    for h in range(heads):
        done = acc_ref[h, 0:HEAD_DIM, :] / acc_ref[h, HEAD_DIM:HEAD_DIM + 1, :]
        for g in range(GROUP):
            head = h * GROUP + g
            block = done[:, g * pad:(g + 1) * pad].T.astype(jnp.bfloat16)
            out_ref[:, head * HEAD_DIM:(head + 1) * HEAD_DIM] = block[0:sel_rows]

    for send in sends:
        send.wait_send()
    for arr in (0, 1):
        kv_copy(arr, core).wait_send()

    def drain_q(i, carry):
        q_copy(chip, i % heads, (i // heads) * 2 + core).wait_send()
        return carry

    lax.fori_loop(0, chip * heads, drain_q, 0)

    def drain_p(i, carry):
        for copy in p_copies(chip, i % heads, chip + 1 + i // heads):
            copy.wait_send()
        return carry

    lax.fori_loop(0, above * heads, drain_p, 0)


def shards(n, kz, hidden, w_query, w_key, w_value, cached_key, cached_value, doc_lengths, selected):
    tok, width = hidden.shape
    cols = w_key.shape[1]
    qcols = w_query.shape[1]
    sel_rows = selected.shape[0] // n
    docs = doc_lengths.shape[0]
    pad = round_up(sel_rows, LANES)
    heads = cols // HEAD_DIM
    qrows = GROUP * pad
    chips = n // 2
    bf, f32 = jnp.bfloat16, jnp.float32
    dma = pltpu.SemaphoreType.DMA
    any_space = pl.BlockSpec(memory_space=pl.ANY)
    vmem = pl.BlockSpec(memory_space=pltpu.VMEM)
    smem = pl.BlockSpec(memory_space=pltpu.SMEM)
    attended, score = pl.pallas_call(
        functools.partial(kernel, n, kz, docs, sel_rows),
        out_shape=(
            jax.ShapeDtypeStruct((sel_rows, qcols), bf),
            jax.ShapeDtypeStruct((1, tok), f32),
        ),
        in_specs=[any_space] * 6 + [smem] * 2,
        out_specs=(vmem, vmem),
        scratch_shapes=[
            pltpu.VMEM((tok, width), bf),
            pltpu.VMEM((width, qcols), bf),
            pltpu.VMEM((width, cols), bf),
            pltpu.VMEM((width, cols), bf),
            pltpu.VMEM((tok, cols), bf),
            pltpu.VMEM((tok, cols), bf),
            pltpu.VMEM((pad, width), bf),
            pltpu.VMEM((2, heads, tok, HEAD_DIM), bf),
            pltpu.VMEM((2, heads, HEAD_DIM + EXTRA, tok), bf),
            pltpu.VMEM((chips, heads, qrows, HEAD_DIM), bf),
            pltpu.VMEM((chips, heads, HEAD_DIM, qrows), bf),
            pltpu.VMEM((chips, heads, 8, qrows), f32),
            pltpu.VMEM((chips, heads, HEAD_DIM, qrows), bf),
            pltpu.VMEM((chips, heads, 8, qrows), f32),
            pltpu.VMEM((heads, 8, qrows), f32),
            pltpu.VMEM((heads, HEAD_DIM + EXTRA, qrows), f32),
            pltpu.VMEM((tok, pad), f32),
            pltpu.VMEM((tok, LANES), f32),
            pltpu.VMEM((8, tok), f32),
            pltpu.VMEM((kz, 8, tok), f32),
            pltpu.VMEM((n, round_up(docs, 8), 128), f32),
            dma((2 * HID_CHUNKS + 3 + heads,)),
            dma((chips, heads)),
            dma((chips, heads)),
            dma((chips, heads, 2)),
            dma((chips, heads, 2)),
            dma((2,)),
            dma((2,)),
            dma((max(1, kz - 1),)),
            dma((kz,)),
            dma((n - 1,)),
            dma((n,)),
        ],
        compiler_params=pltpu.CompilerParams(
            collective_id=0, has_side_effects=True, vmem_limit_bytes=62 * 1024 * 1024
        ),
        name="blend",
    )(hidden, w_query, w_key, w_value, cached_key, cached_value, doc_lengths, selected)
    return attended, score.reshape(tok)


def solution(mesh):
    return jax.shard_map(
        functools.partial(shards, mesh.shape["seq"], mesh.shape["kvh"]),
        mesh=mesh,
        in_specs=(
            P("seq", None),
            P(None, "kvh"),
            P(None, "kvh"),
            P(None, "kvh"),
            P("seq", "kvh"),
            P("seq", "kvh"),
            P(),
            P(),
        ),
        out_specs=(P("seq", "kvh"), P("seq")),
        check_vma=False,
    )
```

time: 46.9 us -> 37.7 us (0.80)
  the two profiles are of different devices: /device:TPU:7 before, /device:TPU:0 now
where the time goes in v1:
time: 37.7 us; the launch traced here: 37.3 us
  Pallas kernels  33.7 us (89%)
  local copies, waits for them, and re-layouts  1.65 us (4%)
  other arithmetic  1.29 us (3%)
  between operations  0.64 us (2%)
    pallas_call x1, Pallas kernels, shards(): pl.pallas_call(functools.partial(kernel, n, kz, docs, sel_rows), out_shap...  33.7 us
    unnamed x1, local copies, waits for them, and re-layouts  1.65 us
    pallas_call x1, other arithmetic, shards(): pl.pallas_call(functools.partial(kernel, n, kz, docs, sel_rows), out_shap...  1.29 us

profile of v1, /device:TPU:0, one launch (start us, length us, event | category | flops | bytes accessed | tf_op | source)
XLA Modules:
  0.0 37.3 jit_solution(11554876774255169389)
XLA Ops:
  0.6 33.7 %blend.1 = (bf16[120,1024]{1,0:T(8,128)(2,1)}, f32[1,768]{1,0:T(1,128)}) custom-call(bf16[768,4096]{1,0:T(8,128)(2,1)} %hid_hbm.1, bf16[4096,1024]{1,0:T(8,128)(2,1)} %wq_hbm.1, bf16[4096,256]{1,0:T(8,128)(2,1)} %wk_hbm.1, bf16[4096,256]{1,0:T(8,128)(2,1)} %wv_hbm.1, bf16[768,256]{1,0:T(8,128)(2,1)} %ck_hbm.1, bf16[768,256]{1,0:T(8,128)(2,1)} %cv_hbm.1, ...), custom_call_target="tpu_custom_call" | custom-call | tf_op jit(solution)/shard_map/blend/pallas_call | solution.py:410
  34.3 1.3 %reduce = f32[768]{0:T(1024)} reduce(f32[1,768]{1,0:T(1,128)} %get-tuple-element.5, f32[]{:T(128)} %constant), dimensions={0}, to_apply=%get-tuple-element.5.reduce_sub_computation | reduce | bytes 6148 | tf_op jit(solution)/shard_map/blend/pallas_call | solution.py:410
  35.6 1.7 %copy.11 = bf16[120,1024]{1,0:T(8,128)(2,1)} copy(bf16[120,1024]{1,0:T(8,128)(2,1)} %get-tuple-element.8) | data formatting | bytes 491520

commit v2 on v1

v2 whole, which is shorter than its diff:
```python
import functools
import math

import jax
import jax.numpy as jnp
from jax import lax
from jax.experimental import pallas as pl
from jax.experimental.pallas import tpu as pltpu
from jax.sharding import PartitionSpec as P

HEADS = 32
KV_HEADS = 8
HEAD_DIM = 128
GROUP = HEADS // KV_HEADS
EXP_SCALE = HEAD_DIM ** (-0.5) * math.log2(math.e)
MESH = pl.DeviceIdType.MESH
NT = (((1,), (1,)), ((), ()))
LANES = 128
EXTRA = 16
HID_CHUNKS = 4


def round_up(a, b):
    return -(-a // b) * b


def split_chips(chips):
    small = max(a for a in range(1, math.isqrt(chips) + 1) if chips % a == 0)
    return small, chips // small


def kernel(
    n, kz, docs, sel_rows,
    hid_hbm, wq_hbm, wk_hbm, wv_hbm, ck_hbm, cv_hbm, lens_hbm, sel_hbm,
    out_ref, score_ref,
    hid, wq, wk, wv, ck, cv, hq, kall, vall, ksend, vsend, qbuf, pout, pout_stat, pin, pin_stat,
    m_ref, acc_ref, bias_ref, chosen_ref, last_ref, devbuf, docbuf, lens_ref, sel_ref,
    load_sem, q_send, q_recv, p_send, p_recv, mv_send, mv_recv, fw_send, fw_recv,
    z_send, z_recv, doc_send, doc_recv,
):
    tok, width = hid.shape
    heads = wk.shape[1] // HEAD_DIM
    pad = hq.shape[0]
    qrows = GROUP * pad
    qcols = GROUP * HEAD_DIM
    plain = tok - sel_rows
    cut = plain // LANES * LANES
    spans = ((0, cut), (cut, tok - cut), (0, tok))
    rows_a, rows_b = split_chips(n // 2)
    me = lax.axis_index("seq")
    zme = lax.axis_index("kvh")
    core = me % 2
    chip = me // 2
    ia, ib = chip // rows_b, chip % rows_b
    partner = me + 1 - 2 * core
    step = width // HID_CHUNKS
    barrier = pltpu.get_barrier_semaphore()
    for d in range(1, n):
        pl.semaphore_signal(barrier, inc=1, device_id={"seq": (me + d) % n}, device_id_type=MESH)
    for d in range(1, kz):
        pl.semaphore_signal(barrier, inc=1, device_id={"kvh": (zme + d) % kz}, device_id_type=MESH)

    loads = []

    def load(src, dst):
        copy = pltpu.make_async_copy(src, dst, load_sem.at[len(loads)])
        copy.start()
        loads.append(copy)
        return copy

    sel_load = load(sel_hbm, sel_ref)
    lens_load = load(lens_hbm, lens_ref)
    ck_load = load(ck_hbm, ck)
    cv_load = load(cv_hbm, cv)
    hid_loads, wq_loads = [], []
    for c in range(HID_CHUNKS):
        part = pl.ds(c * step, step)
        hid_loads.append(load(hid_hbm.at[:, part], hid.at[:, part]))
        wq_loads.append(load(wq_hbm.at[part, pl.ds(0, qcols)], wq.at[part, pl.ds(0, qcols)]))
    rest_loads = [
        load(wq_hbm.at[:, pl.ds(h * qcols, qcols)], wq.at[:, pl.ds(h * qcols, qcols)])
        for h in range(1, heads)
    ]
    wk_load = load(wk_hbm, wk)
    wv_load = load(wv_hbm, wv)

    def axes(h):
        if h % 2 == 0:
            return ib, rows_b, ia, rows_a
        return ia, rows_a, ib, rows_b

    def chip_at(h, q, k):
        return k * rows_b + q if h % 2 == 0 else q * rows_b + k

    def sends_kv(h, to):
        qc, nq, kc, nk = axes(h)
        if h % 2 == 0:
            return to > kc
        return (to != kc) & ((qc < nq - 1) | (to > kc))

    def takes_kv(h, source):
        qc, nq, kc, nk = axes(h)
        if h % 2 == 0:
            return source < kc
        return (source != kc) & ((qc < nq - 1) | (source < kc))

    def sends_q(h, to):
        qc, nq, kc, nk = axes(h)
        if h % 2 == 0:
            return (to != qc) & ((to < qc) | (kc > 0))
        return to < qc

    def takes_q(h, source):
        qc, nq, kc, nk = axes(h)
        if h % 2 == 0:
            return (source != qc) & ((source > qc) | (kc > 0))
        return source > qc

    def each(count, want, body):
        def go(i, carry):
            pl.when(want(i))(functools.partial(body, i))
            return carry
        lax.fori_loop(0, count, go, 0)

    def block(arr, h, slot, which, span):
        first, rows = spans[span]
        if arr == 0:
            return kall.at[h, slot, which, pl.ds(first, rows)]
        return vall.at[h, slot, which, pl.ds(0, HEAD_DIM), pl.ds(first, rows)]

    def move(arr, h, span, to):
        qc, nq, kc, nk = axes(h)
        first, rows = spans[span]
        src = ksend.at[h, pl.ds(first, rows)] if arr == 0 else vsend.at[h, :, pl.ds(first, rows)]
        return pltpu.make_async_remote_copy(
            src_ref=src, dst_ref=block(arr, h, kc, core, span),
            send_sem=mv_send.at[h, to, span, arr], recv_sem=mv_recv.at[h, kc, span, arr],
            device_id={"seq": chip_at(h, qc, to) * 2 + core}, device_id_type=MESH,
        )

    def moved(arr, h, span, source):
        view = block(arr, h, source, core, span)
        return pltpu.make_async_remote_copy(
            src_ref=view, dst_ref=view, send_sem=mv_send.at[h, source, span, arr],
            recv_sem=mv_recv.at[h, source, span, arr],
            device_id={"seq": partner}, device_id_type=MESH,
        )

    def forward(arr, h, slot, which, span):
        view = block(arr, h, slot, which, span)
        return pltpu.make_async_remote_copy(
            src_ref=view, dst_ref=view, send_sem=fw_send.at[h, slot, span % 2, arr],
            recv_sem=fw_recv.at[h, slot, span % 2, arr],
            device_id={"seq": partner}, device_id_type=MESH,
        )

    def send_blocks(span):
        for h in range(heads):
            def go(to, h=h):
                for arr in (0, 1):
                    move(arr, h, span, to).start()
            each(axes(h)[3], functools.partial(sends_kv, h), go)

    def forward_blocks(span):
        for h in range(heads):
            def go(source, h=h):
                for arr in (0, 1):
                    moved(arr, h, span, source).wait_recv()
                    forward(arr, h, source, core, span).start()
            each(axes(h)[3], functools.partial(takes_kv, h), go)

    for h in range(heads):
        for i in range(kall.shape[1]):
            for c in range(2):
                vall[h, i, c, HEAD_DIM:, :] = jnp.ones((EXTRA, tok), jnp.bfloat16)
        for j in range(m_ref.shape[1]):
            m_ref[h, j] = jnp.full(m_ref.shape[2:], -1e30, jnp.float32)
            acc_ref[h, j] = jnp.zeros(acc_ref.shape[2:], jnp.float32)

    slot = lax.broadcasted_iota(jnp.int32, (8, pad), 1)
    sel_load.wait()

    def place(r, row):
        return jnp.where(slot == r, sel_ref[me * sel_rows + r], row)

    row_pos = lax.fori_loop(0, sel_rows, place, jnp.full((8, pad), -1, jnp.int32), unroll=8)[0:1]
    row_col = jnp.broadcast_to(row_pos.astype(jnp.float32), (LANES, pad)).T
    lane = lax.broadcasted_iota(jnp.int32, (pad, LANES), 1).astype(jnp.float32)
    pick = jnp.concatenate(
        [
            jnp.where(row_col == lane + float(k * LANES), 1.0, 0.0).astype(jnp.bfloat16)
            for k in range(tok // LANES)
        ],
        axis=1,
    )
    key_row = lax.broadcasted_iota(jnp.int32, (tok, pad), 0)
    pick_t = jnp.where(key_row == row_pos, 1.0, 0.0).astype(jnp.bfloat16)
    chosen_ref[...] = jnp.dot(
        pick_t, jnp.ones((pad, LANES), jnp.bfloat16), preferred_element_type=jnp.float32
    )
    bias_ref[...] = jnp.where(key_row <= row_pos, 0.0, -1e30)

    chosen = jnp.dot(jnp.ones((16, pad), jnp.bfloat16), pick, preferred_element_type=jnp.float32)
    upper = (
        lax.broadcasted_iota(jnp.int32, (LANES, LANES), 0)
        <= lax.broadcasted_iota(jnp.int32, (LANES, LANES), 1)
    ).astype(jnp.float32).astype(jnp.bfloat16)
    counts, before = [], jnp.zeros((1, 1), jnp.float32)
    for k in range(tok // LANES):
        tile = chosen[:, k * LANES:(k + 1) * LANES].astype(jnp.bfloat16)
        inner = jnp.dot(tile, upper, preferred_element_type=jnp.float32)[0:1]
        counts.append(inner + before)
        before = before + inner[:, LANES - 1:LANES]
    count = jnp.concatenate(counts, axis=1).astype(jnp.int32)
    token = lax.broadcasted_iota(jnp.int32, (1, tok), 1)
    target = jnp.where(chosen[0:1] > 0.5, plain + count - 1, token - count)

    def order(first, rows):
        row = lax.broadcasted_iota(jnp.int32, (rows, tok), 0) + first
        return jnp.where(row == target, 1.0, 0.0).astype(jnp.bfloat16)

    last_ref[...] = order(cut, tok - cut)
    early = order(0, cut)
    ck_load.wait()
    cv_load.wait()
    keys = jnp.dot(early, ck[...], preferred_element_type=jnp.float32).astype(jnp.bfloat16)
    values = jnp.dot(early, cv[...], preferred_element_type=jnp.float32)
    for h in range(heads):
        part = slice(h * HEAD_DIM, (h + 1) * HEAD_DIM)
        ksend[h, 0:cut, :] = keys[:, part]
        vsend[h, :, 0:cut] = values[:, part].T.astype(jnp.bfloat16)

    def q_copy(h, to):
        qc, nq, kc, nk = axes(h)
        view = qbuf.at[h, qc]
        return pltpu.make_async_remote_copy(
            src_ref=view, dst_ref=view, send_sem=q_send.at[h, to], recv_sem=q_recv.at[h, qc],
            device_id={"seq": chip_at(h, to, kc) * 2 + core}, device_id_type=MESH,
        )

    def q_wait(h, source):
        view = qbuf.at[h, source]
        pltpu.make_async_remote_copy(
            src_ref=view, dst_ref=view, send_sem=q_send.at[h, source],
            recv_sem=q_recv.at[h, source], device_id={"seq": partner}, device_id_type=MESH,
        ).wait_recv()

    def send_queries(h, queries):
        qc, nq, kc, nk = axes(h)
        scaled = (queries * EXP_SCALE).astype(jnp.bfloat16)
        for g in range(GROUP):
            qbuf[h, qc, g * pad:(g + 1) * pad, :] = scaled[:, g * HEAD_DIM:(g + 1) * HEAD_DIM]
        each(nq, functools.partial(sends_q, h), lambda to: q_copy(h, to).start())

    queries = jnp.zeros((pad, qcols), jnp.float32)
    for c in range(HID_CHUNKS):
        part = slice(c * step, (c + 1) * step)
        hid_loads[c].wait()
        picked = jnp.dot(pick, hid[:, part], preferred_element_type=jnp.float32)
        picked = picked.astype(jnp.bfloat16)
        hq[:, part] = picked
        wq_loads[c].wait()
        queries = queries + jnp.dot(picked, wq[part, 0:qcols], preferred_element_type=jnp.float32)
        if c == min(1, HID_CHUNKS - 1):
            pl.semaphore_wait(barrier, n - 1 + kz - 1)
            send_blocks(0)
    send_queries(0, queries)
    for h in range(1, heads):
        rest_loads[h - 1].wait()
        send_queries(
            h,
            jnp.dot(
                hq[...], wq[:, h * qcols:(h + 1) * qcols], preferred_element_type=jnp.float32
            ),
        )

    pieces = 2 if tok % (2 * LANES) == 0 else 1
    half = tok // pieces

    def fold(shift):
        square = shift * shift
        folded = square[:, 0:HEAD_DIM]
        for h in range(1, heads):
            folded = folded + square[:, h * HEAD_DIM:(h + 1) * HEAD_DIM]
        return jnp.sum(folded.T, axis=0, keepdims=True)
    wk_load.wait()
    key_dev = []
    for p in range(pieces):
        rows = slice(p * half, (p + 1) * half)
        fresh = jnp.dot(hid[rows, :], wk[...], preferred_element_type=jnp.float32)
        cached = ck[rows, :].astype(jnp.float32)
        key_dev.append(fold(fresh - cached))
        mask = jnp.concatenate([chosen_ref[rows, :]] * heads, axis=1) > 0.5
        used = jnp.where(mask, fresh, cached).astype(jnp.bfloat16)
        for h in range(heads):
            kall[h, axes(h)[2], core, rows, :] = used[:, h * HEAD_DIM:(h + 1) * HEAD_DIM]
    for h in range(heads):
        forward(0, h, axes(h)[2], core, 2).start()
        ksend[h, cut:tok, :] = jnp.dot(
            last_ref[...], kall[h, axes(h)[2], core], preferred_element_type=jnp.float32
        ).astype(jnp.bfloat16)
    wv_load.wait()
    for p in range(pieces):
        rows = slice(p * half, (p + 1) * half)
        fresh = jnp.dot(hid[rows, :], wv[...], preferred_element_type=jnp.float32)
        cached = cv[rows, :].astype(jnp.float32)
        devbuf[zme, :, rows] = key_dev[p] + fold(fresh - cached)
        mask = jnp.concatenate([chosen_ref[rows, :]] * heads, axis=1) > 0.5
        used = jnp.where(mask, fresh, cached).T.astype(jnp.bfloat16)
        for h in range(heads):
            vall[h, axes(h)[2], core, 0:HEAD_DIM, rows] = used[h * HEAD_DIM:(h + 1) * HEAD_DIM, :]
    for h in range(heads):
        forward(1, h, axes(h)[2], core, 2).start()
        vsend[h, :, cut:tok] = lax.dot_general(
            vall[h, axes(h)[2], core, 0:HEAD_DIM, :], last_ref[...], NT,
            preferred_element_type=jnp.float32,
        ).astype(jnp.bfloat16)
    send_blocks(1)
    sends = []
    for d in range(1, kz):
        sends.append(
            pltpu.make_async_remote_copy(
                src_ref=devbuf.at[zme], dst_ref=devbuf.at[zme], send_sem=z_send.at[d - 1],
                recv_sem=z_recv.at[zme], device_id={"kvh": (zme + d) % kz}, device_id_type=MESH,
            )
        )
        sends[-1].start()

    cols = 2 * LANES if qrows % (2 * LANES) == 0 else LANES
    col_parts = [slice(j, j + cols) for j in range(0, qrows, cols)]

    def run(items):
        def scores_of(item):
            h, q, k, which, part, masked = item
            s = lax.dot_general(
                kall[h, k, which], qbuf[h, q, part, :], NT, preferred_element_type=jnp.float32
            )
            if masked:
                first = part.start % pad
                if cols <= pad:
                    bias = bias_ref[:, first:first + cols]
                else:
                    bias = jnp.concatenate([bias_ref[...]] * (cols // pad), axis=1)
                s = s + bias
            return s

        scores = scores_of(items[0])
        for i, (h, q, k, which, part, masked) in enumerate(items):
            following = scores_of(items[i + 1]) if i + 1 < len(items) else None
            best = jnp.max(scores, axis=0, keepdims=True)
            weights = jnp.exp2(scores - best).astype(jnp.bfloat16)
            mixed = jnp.dot(vall[h, k, which], weights, preferred_element_type=jnp.float32)
            if not masked:
                old = m_ref[h, q, 0:1, part]
                top = jnp.maximum(old, best)
                mixed = mixed * jnp.exp2(best - top)
                mixed = mixed + acc_ref[h, q, :, part] * jnp.exp2(old - top)
                best = top
            m_ref[h, q, 0:1, part] = best
            acc_ref[h, q, :, part] = mixed
            scores = following

    def both(h, q, k):
        run([(h, q, k, c, part, False) for part in col_parts for c in (core, 1 - core)])

    def p_copies(h, to):
        qc, nq, kc, nk = axes(h)
        dest = {"seq": chip_at(h, to, kc) * 2 + core}
        return [
            pltpu.make_async_remote_copy(
                src_ref=pout.at[h, to], dst_ref=pin.at[h, qc], send_sem=p_send.at[h, to, 0],
                recv_sem=p_recv.at[h, qc, 0], device_id=dest, device_id_type=MESH,
            ),
            pltpu.make_async_remote_copy(
                src_ref=pout_stat.at[h, to], dst_ref=pin_stat.at[h, qc],
                send_sem=p_send.at[h, to, 1], recv_sem=p_recv.at[h, qc, 1],
                device_id=dest, device_id_type=MESH,
            ),
        ]

    def p_wait(h, source):
        for i, buf in enumerate((pin, pin_stat)):
            view = buf.at[h, source]
            pltpu.make_async_remote_copy(
                src_ref=view, dst_ref=view, send_sem=p_send.at[h, source, i],
                recv_sem=p_recv.at[h, source, i], device_id={"seq": partner}, device_id_type=MESH,
            ).wait_recv()

    def give_back(h, to):
        pout[h, to] = acc_ref[h, to, 0:HEAD_DIM, :].astype(jnp.bfloat16)
        pout_stat[h, to, 0:1, :] = m_ref[h, to, 0:1, :]
        pout_stat[h, to, 1:2, :] = acc_ref[h, to, HEAD_DIM:HEAD_DIM + 1, :]
        for copy in p_copies(h, to):
            copy.start()

    def no_moved(h):
        qc, nq, kc, nk = axes(h)
        return kc == 0 if h % 2 == 0 else nk == 1
    run(
        [
            (h, axes(h)[0], axes(h)[2], core, part, True)
            for h in range(heads)
            for part in col_parts
        ]
    )
    forward_blocks(0)
    for h in range(heads):
        for arr in (0, 1):
            forward(arr, h, axes(h)[2], 1 - core, 2).wait_recv()
    for h in range(heads):
        def serve_own(j, h=h):
            q_wait(h, j)
            both(h, j, axes(h)[2])
            pl.when(no_moved(h))(lambda: give_back(h, j))
        each(axes(h)[1], lambda j, h=h: j > axes(h)[0], serve_own)
    forward_blocks(1)
    @pl.when(core == 1)
    def _():
        run(
            [
                (h, axes(h)[0], axes(h)[2], 0, part, False)
                for h in range(heads)
                for part in col_parts
            ]
        )
    for h in range(heads):
        def arrive(source, h=h):
            for span in (0, 1):
                for arr in (0, 1):
                    forward(arr, h, source, 1 - core, span).wait_recv()
        each(axes(h)[3], functools.partial(takes_kv, h), arrive)
    for h in range(heads):
        qc, nq, kc, nk = axes(h)

        def serve_moved(j, h=h, qc=qc, nk=nk):
            pl.when(j < qc)(lambda: q_wait(h, j))
            each(nk, functools.partial(takes_kv, h), lambda i: both(h, j, i))
            give_back(h, j)

        each(
            nq,
            lambda j, h=h: takes_q(h, j) & jnp.logical_not(no_moved(h)),
            serve_moved,
        )
    for h in range(heads):
        qc, nq, kc, nk = axes(h)
        each(nk, lambda i, kc=kc: i < kc, lambda i, h=h, qc=qc: both(h, qc, i))
    for d in range(1, kz):
        src = (zme + d) % kz
        pltpu.make_async_remote_copy(
            src_ref=devbuf.at[src], dst_ref=devbuf.at[src], send_sem=z_send.at[0],
            recv_sem=z_recv.at[src], device_id={"kvh": src}, device_id_type=MESH,
        ).wait_recv()
    lens_load.wait()
    deviation = devbuf[0]
    for z in range(1, kz):
        deviation = deviation + devbuf[z]
    position = token + me * tok
    inside = []
    end = jnp.int32(0)
    for d in range(docs):
        begin, end = end, end + lens_ref[d]
        inside.append((position >= begin) & (position < end))
    slot_row = lax.broadcasted_iota(jnp.int32, docbuf.shape[1:], 0)
    shares = jnp.zeros(docbuf.shape[1:], jnp.float32)
    for d in range(docs):
        share = jnp.sum(jnp.where(inside[d], deviation, 0.0), axis=1, keepdims=True)
        shares = jnp.where(slot_row == d, share, shares)
    docbuf[me] = shares
    for d in range(1, n):
        sends.append(
            pltpu.make_async_remote_copy(
                src_ref=docbuf.at[me], dst_ref=docbuf.at[me], send_sem=doc_send.at[d - 1],
                recv_sem=doc_recv.at[me], device_id={"seq": (me + d) % n}, device_id_type=MESH,
            )
        )
        sends[-1].start()
    for h in range(heads):
        qc, nq, kc, nk = axes(h)

        def collect(source, h=h, qc=qc):
            p_wait(h, source)
            best = m_ref[h, qc, 0:1, :]
            other = pin_stat[h, source, 0:1, :]
            top = jnp.maximum(best, other)
            fade, rise = jnp.exp2(best - top), jnp.exp2(other - top)
            m_ref[h, qc, 0:1, :] = top
            acc_ref[h, qc, 0:HEAD_DIM, :] = (
                acc_ref[h, qc, 0:HEAD_DIM, :] * fade + pin[h, source].astype(jnp.float32) * rise
            )
            acc_ref[h, qc, HEAD_DIM:HEAD_DIM + 1, :] = (
                acc_ref[h, qc, HEAD_DIM:HEAD_DIM + 1, :] * fade + pin_stat[h, source, 1:2, :] * rise
            )

        each(nq, functools.partial(sends_q, h), collect)
        done = acc_ref[h, qc, 0:HEAD_DIM, :] / acc_ref[h, qc, HEAD_DIM:HEAD_DIM + 1, :]
        for g in range(GROUP):
            head = h * GROUP + g
            rows = done[:, g * pad:(g + 1) * pad].T.astype(jnp.bfloat16)
            out_ref[:, head * HEAD_DIM:(head + 1) * HEAD_DIM] = rows[0:sel_rows]
    for d in range(1, n):
        src = (me + d) % n
        pltpu.make_async_remote_copy(
            src_ref=docbuf.at[src], dst_ref=docbuf.at[src], send_sem=doc_send.at[0],
            recv_sem=doc_recv.at[src], device_id={"seq": src}, device_id_type=MESH,
        ).wait_recv()
    totals = docbuf[0]
    for s in range(1, n):
        totals = totals + docbuf[s]
    mean = jnp.zeros((1, tok), jnp.float32)
    for d in range(docs):
        here = totals[d:d + 1, 0:1] / lens_ref[d].astype(jnp.float32)
        mean = jnp.where(inside[d], here, mean)
    score_ref[...] = deviation / (mean + 1.0)
    for send in sends:
        send.wait_send()
    for h in range(heads):
        qc, nq, kc, nk = axes(h)

        def drain_kv(to, h=h):
            for span in (0, 1):
                for arr in (0, 1):
                    move(arr, h, span, to).wait_send()

        def drain_forward(source, h=h):
            for span in (0, 1):
                for arr in (0, 1):
                    forward(arr, h, source, core, span).wait_send()

        def drain_p(to, h=h):
            for copy in p_copies(h, to):
                copy.wait_send()

        for arr in (0, 1):
            forward(arr, h, kc, core, 2).wait_send()
        each(nk, functools.partial(sends_kv, h), drain_kv)
        each(nk, functools.partial(takes_kv, h), drain_forward)
        each(nq, functools.partial(sends_q, h), lambda to, h=h: q_copy(h, to).wait_send())
        each(nq, functools.partial(takes_q, h), drain_p)


def shards(n, kz, hidden, w_query, w_key, w_value, cached_key, cached_value, doc_lengths, selected):
    tok, width = hidden.shape
    cols = w_key.shape[1]
    qcols = w_query.shape[1]
    sel_rows = selected.shape[0] // n
    docs = doc_lengths.shape[0]
    pad = round_up(sel_rows, LANES)
    heads = cols // HEAD_DIM
    qrows = GROUP * pad
    cut = (tok - sel_rows) // LANES * LANES
    side = max(split_chips(n // 2))
    bf, f32 = jnp.bfloat16, jnp.float32
    dma = pltpu.SemaphoreType.DMA
    any_space = pl.BlockSpec(memory_space=pl.ANY)
    vmem = pl.BlockSpec(memory_space=pltpu.VMEM)
    attended, score = pl.pallas_call(
        functools.partial(kernel, n, kz, docs, sel_rows),
        out_shape=(
            jax.ShapeDtypeStruct((sel_rows, qcols), bf),
            jax.ShapeDtypeStruct((1, tok), f32),
        ),
        in_specs=[any_space] * 8,
        out_specs=(vmem, vmem),
        scratch_shapes=[
            pltpu.VMEM((tok, width), bf),
            pltpu.VMEM((width, qcols), bf),
            pltpu.VMEM((width, cols), bf),
            pltpu.VMEM((width, cols), bf),
            pltpu.VMEM((tok, cols), bf),
            pltpu.VMEM((tok, cols), bf),
            pltpu.VMEM((pad, width), bf),
            pltpu.VMEM((heads, side, 2, tok, HEAD_DIM), bf),
            pltpu.VMEM((heads, side, 2, HEAD_DIM + EXTRA, tok), bf),
            pltpu.VMEM((heads, tok, HEAD_DIM), bf),
            pltpu.VMEM((heads, HEAD_DIM, tok), bf),
            pltpu.VMEM((heads, side, qrows, HEAD_DIM), bf),
            pltpu.VMEM((heads, side, HEAD_DIM, qrows), bf),
            pltpu.VMEM((heads, side, 2, qrows), f32),
            pltpu.VMEM((heads, side, HEAD_DIM, qrows), bf),
            pltpu.VMEM((heads, side, 2, qrows), f32),
            pltpu.VMEM((heads, side, 8, qrows), f32),
            pltpu.VMEM((heads, side, HEAD_DIM + EXTRA, qrows), f32),
            pltpu.VMEM((tok, pad), f32),
            pltpu.VMEM((tok, LANES), f32),
            pltpu.VMEM((tok - cut, tok), bf),
            pltpu.VMEM((kz, 1, tok), f32),
            pltpu.VMEM((n, round_up(docs, 8), 128), f32),
            pltpu.SMEM(doc_lengths.shape, jnp.int32),
            pltpu.SMEM(selected.shape, jnp.int32),
            dma((2 * HID_CHUNKS + 5 + heads,)),
            dma((heads, side)),
            dma((heads, side)),
            dma((heads, side, 2)),
            dma((heads, side, 2)),
            dma((heads, side, 2, 2)),
            dma((heads, side, 2, 2)),
            dma((heads, side, 2, 2)),
            dma((heads, side, 2, 2)),
            dma((max(1, kz - 1),)),
            dma((kz,)),
            dma((n - 1,)),
            dma((n,)),
        ],
        compiler_params=pltpu.CompilerParams(
            collective_id=0, has_side_effects=True, vmem_limit_bytes=62 * 1024 * 1024
        ),
        name="blend",
    )(hidden, w_query, w_key, w_value, cached_key, cached_value, doc_lengths, selected)
    return attended, score.reshape(tok)


def solution(mesh):
    return jax.shard_map(
        functools.partial(shards, mesh.shape["seq"], mesh.shape["kvh"]),
        mesh=mesh,
        in_specs=(
            P("seq", None),
            P(None, "kvh"),
            P(None, "kvh"),
            P(None, "kvh"),
            P("seq", "kvh"),
            P("seq", "kvh"),
            P(),
            P(),
        ),
        out_specs=(P("seq", "kvh"), P("seq")),
        check_vma=False,
    )
```

time: 37.7 us -> 32.4 us (0.86)
  Pallas kernels: 33.7 us -> 28.6 us
    pallas_call x1, Pallas kernels: 33.7 us -> 28.6 us  [shards(): pl.pallas_call(functools.partial(kernel, n, kz, docs, sel_rows), out_shap...]
where the time goes in v2:
time: 32.4 us; the launch traced here: 32.2 us
  Pallas kernels  28.6 us (88%)
  local copies, waits for them, and re-layouts  1.65 us (5%)
  other arithmetic  1.29 us (4%)
  between operations  0.64 us (2%)
    pallas_call x1, Pallas kernels, shards(): pl.pallas_call(functools.partial(kernel, n, kz, docs, sel_rows), out_shap...  28.6 us
    unnamed x1, local copies, waits for them, and re-layouts  1.65 us
    pallas_call x1, other arithmetic, shards(): pl.pallas_call(functools.partial(kernel, n, kz, docs, sel_rows), out_shap...  1.29 us

profile of v2, /device:TPU:0, one launch (start us, length us, event | category | flops | bytes accessed | tf_op | source)
XLA Modules:
  0.0 32.2 jit_solution(1441838259320111464)
XLA Ops:
  0.6 28.6 %blend.1 = (bf16[120,1024]{1,0:T(8,128)(2,1)}, f32[1,768]{1,0:T(1,128)}) custom-call(bf16[768,4096]{1,0:T(8,128)(2,1)} %hid_hbm.1, bf16[4096,1024]{1,0:T(8,128)(2,1)} %wq_hbm.1, bf16[4096,256]{1,0:T(8,128)(2,1)} %wk_hbm.1, bf16[4096,256]{1,0:T(8,128)(2,1)} %wv_hbm.1, bf16[768,256]{1,0:T(8,128)(2,1)} %ck_hbm.1, bf16[768,256]{1,0:T(8,128)(2,1)} %cv_hbm.1, ...), custom_call_target="tpu_custom_call" | custom-call | tf_op jit(solution)/shard_map/blend/pallas_call | solution.py:557
  29.3 1.3 %reduce = f32[768]{0:T(1024)} reduce(f32[1,768]{1,0:T(1,128)} %get-tuple-element.5, f32[]{:T(128)} %constant), dimensions={0}, to_apply=%get-tuple-element.5.reduce_sub_computation | reduce | bytes 6148 | tf_op jit(solution)/shard_map/blend/pallas_call | solution.py:557
  30.5 1.7 %copy.11 = bf16[120,1024]{1,0:T(8,128)(2,1)} copy(bf16[120,1024]{1,0:T(8,128)(2,1)} %get-tuple-element.8) | data formatting | bytes 491520

commit v3 on v2

--- a/solution.py
+++ b/solution.py
@@ -24,6 +24,10 @@
     return -(-a // b) * b
 
 
+def q_cols(rows):
+    return 2 * LANES if rows % (2 * LANES) == 0 else LANES
+
+
 def split_chips(chips):
     small = max(a for a in range(1, math.isqrt(chips) + 1) if chips % a == 0)
     return small, chips // small
@@ -34,8 +38,8 @@
     hid_hbm, wq_hbm, wk_hbm, wv_hbm, ck_hbm, cv_hbm, lens_hbm, sel_hbm,
     out_ref, score_ref,
     hid, wq, wk, wv, ck, cv, hq, kall, vall, ksend, vsend, qbuf, pout, pout_stat, pin, pin_stat,
-    m_ref, acc_ref, bias_ref, chosen_ref, last_ref, devbuf, docbuf, lens_ref, sel_ref,
-    load_sem, q_send, q_recv, p_send, p_recv, mv_send, mv_recv, fw_send, fw_recv,
+    kacc, vacc, m_ref, acc_ref, bias_ref, chosen_ref, last_ref, devbuf, docbuf, lens_ref, sel_ref,
+    load_sem, q_send, q_recv, p_send, p_recv, mv_send, mv_recv, fw_send, fw_recv, own_send, own_recv,
     z_send, z_recv, doc_send, doc_recv,
 ):
     tok, width = hid.shape
@@ -69,20 +73,24 @@
         return copy
 
     sel_load = load(sel_hbm, sel_ref)
-    lens_load = load(lens_hbm, lens_ref)
     ck_load = load(ck_hbm, ck)
     cv_load = load(cv_hbm, cv)
-    hid_loads, wq_loads = [], []
+    lens_load = load(lens_hbm, lens_ref)
+    chunk_loads = []
     for c in range(HID_CHUNKS):
         part = pl.ds(c * step, step)
-        hid_loads.append(load(hid_hbm.at[:, part], hid.at[:, part]))
-        wq_loads.append(load(wq_hbm.at[part, pl.ds(0, qcols)], wq.at[part, pl.ds(0, qcols)]))
-    rest_loads = [
-        load(wq_hbm.at[:, pl.ds(h * qcols, qcols)], wq.at[:, pl.ds(h * qcols, qcols)])
-        for h in range(1, heads)
-    ]
-    wk_load = load(wk_hbm, wk)
-    wv_load = load(wv_hbm, wv)
+        chunk_loads.append(
+            (
+                load(hid_hbm.at[:, part], hid.at[:, part]),
+                load(wk_hbm.at[part], wk.at[part]),
+                load(wv_hbm.at[part], wv.at[part]),
+            )
+        )
+    head_order = sorted(range(heads), key=lambda h: (1 - h % 2, h))
+    wq_loads = {
+        h: load(wq_hbm.at[:, pl.ds(h * qcols, qcols)], wq.at[:, pl.ds(h * qcols, qcols)])
+        for h in head_order
+    }
 
     def axes(h):
         if h % 2 == 0:
@@ -134,40 +142,57 @@
         src = ksend.at[h, pl.ds(first, rows)] if arr == 0 else vsend.at[h, :, pl.ds(first, rows)]
         return pltpu.make_async_remote_copy(
             src_ref=src, dst_ref=block(arr, h, kc, core, span),
-            send_sem=mv_send.at[h, to, span, arr], recv_sem=mv_recv.at[h, kc, span, arr],
+            send_sem=mv_send.at[h, (to - kc - 1) % nk, span, arr],
+            recv_sem=mv_recv.at[h, (kc - to - 1) % nk, span, arr],
             device_id={"seq": chip_at(h, qc, to) * 2 + core}, device_id_type=MESH,
         )
 
     def moved(arr, h, span, source):
+        qc, nq, kc, nk = axes(h)
+        index = (source - kc - 1) % nk
         view = block(arr, h, source, core, span)
         return pltpu.make_async_remote_copy(
-            src_ref=view, dst_ref=view, send_sem=mv_send.at[h, source, span, arr],
-            recv_sem=mv_recv.at[h, source, span, arr],
+            src_ref=view, dst_ref=view, send_sem=mv_send.at[h, index, span, arr],
+            recv_sem=mv_recv.at[h, index, span, arr],
             device_id={"seq": partner}, device_id_type=MESH,
         )
 
     def forward(arr, h, slot, which, span):
+        qc, nq, kc, nk = axes(h)
         view = block(arr, h, slot, which, span)
+        if span == 2:
+            send_sem, recv_sem = own_send.at[h, arr], own_recv.at[h, arr]
+        else:
+            index = (slot - kc - 1) % nk
+            send_sem, recv_sem = fw_send.at[h, index, span, arr], fw_recv.at[h, index, span, arr]
         return pltpu.make_async_remote_copy(
-            src_ref=view, dst_ref=view, send_sem=fw_send.at[h, slot, span % 2, arr],
-            recv_sem=fw_recv.at[h, slot, span % 2, arr],
+            src_ref=view, dst_ref=view, send_sem=send_sem, recv_sem=recv_sem,
             device_id={"seq": partner}, device_id_type=MESH,
         )
 
-    def send_blocks(span):
+    def send_blocks(arr, span):
         for h in range(heads):
             def go(to, h=h):
+                move(arr, h, span, to).start()
+            each(axes(h)[3], functools.partial(sends_kv, h), go)
+
+    def shared_link(h, source):
+        qc, nq, kc, nk = axes(h)
+        return (source > kc) | (qc == nq - 1)
+
+    def forward_blocks(h, span, want):
+        def go(source):
+            for arr in (0, 1):
+                moved(arr, h, span, source).wait_recv()
+                forward(arr, h, source, core, span).start()
+        each(axes(h)[3], want, go)
+
+    def arrive(h):
+        def go(source):
+            for span in (0, 1):
                 for arr in (0, 1):
-                    move(arr, h, span, to).start()
-            each(axes(h)[3], functools.partial(sends_kv, h), go)
-
-    def forward_blocks(span):
-        for h in range(heads):
-            def go(source, h=h):
-                for arr in (0, 1):
-                    moved(arr, h, span, source).wait_recv()
-                    forward(arr, h, source, core, span).start()
-            each(axes(h)[3], functools.partial(takes_kv, h), go)
+                    forward(arr, h, source, 1 - core, span).wait_recv()
+        each(axes(h)[3], functools.partial(takes_kv, h), go)
 
     for h in range(heads):
         for i in range(kall.shape[1]):
@@ -184,6 +209,8 @@
         return jnp.where(slot == r, sel_ref[me * sel_rows + r], row)
 
     row_pos = lax.fori_loop(0, sel_rows, place, jnp.full((8, pad), -1, jnp.int32), unroll=8)[0:1]
+    ck_load.wait()
+    cv_load.wait()
     row_col = jnp.broadcast_to(row_pos.astype(jnp.float32), (LANES, pad)).T
     lane = lax.broadcasted_iota(jnp.int32, (pad, LANES), 1).astype(jnp.float32)
     pick = jnp.concatenate(
@@ -221,8 +248,6 @@
 
     last_ref[...] = order(cut, tok - cut)
     early = order(0, cut)
-    ck_load.wait()
-    cv_load.wait()
     keys = jnp.dot(early, ck[...], preferred_element_type=jnp.float32).astype(jnp.bfloat16)
     values = jnp.dot(early, cv[...], preferred_element_type=jnp.float32)
     for h in range(heads):
@@ -230,19 +255,25 @@
         ksend[h, 0:cut, :] = keys[:, part]
         vsend[h, :, 0:cut] = values[:, part].T.astype(jnp.bfloat16)
 
-    def q_copy(h, to):
-        qc, nq, kc, nk = axes(h)
-        view = qbuf.at[h, qc]
+    cols = q_cols(qrows)
+    col_parts = [slice(j, j + cols) for j in range(0, qrows, cols)]
+
+    def q_copy(h, to, index):
+        qc, nq, kc, nk = axes(h)
+        view = qbuf.at[h, qc, pl.ds(index * cols, cols)]
         return pltpu.make_async_remote_copy(
-            src_ref=view, dst_ref=view, send_sem=q_send.at[h, to], recv_sem=q_recv.at[h, qc],
+            src_ref=view, dst_ref=view, send_sem=q_send.at[h, (to - qc - 1) % nq, index],
+            recv_sem=q_recv.at[h, (qc - to - 1) % nq, index],
             device_id={"seq": chip_at(h, to, kc) * 2 + core}, device_id_type=MESH,
         )
 
-    def q_wait(h, source):
-        view = qbuf.at[h, source]
+    def q_wait(h, source, index):
+        qc, nq, kc, nk = axes(h)
+        place = (source - qc - 1) % nq
+        view = qbuf.at[h, source, pl.ds(index * cols, cols)]
         pltpu.make_async_remote_copy(
-            src_ref=view, dst_ref=view, send_sem=q_send.at[h, source],
-            recv_sem=q_recv.at[h, source], device_id={"seq": partner}, device_id_type=MESH,
+            src_ref=view, dst_ref=view, send_sem=q_send.at[h, place, index],
+            recv_sem=q_recv.at[h, place, index], device_id={"seq": partner}, device_id_type=MESH,
         ).wait_recv()
 
     def send_queries(h, queries):
@@ -250,29 +281,12 @@
         scaled = (queries * EXP_SCALE).astype(jnp.bfloat16)
         for g in range(GROUP):
             qbuf[h, qc, g * pad:(g + 1) * pad, :] = scaled[:, g * HEAD_DIM:(g + 1) * HEAD_DIM]
-        each(nq, functools.partial(sends_q, h), lambda to: q_copy(h, to).start())
-
-    queries = jnp.zeros((pad, qcols), jnp.float32)
-    for c in range(HID_CHUNKS):
-        part = slice(c * step, (c + 1) * step)
-        hid_loads[c].wait()
-        picked = jnp.dot(pick, hid[:, part], preferred_element_type=jnp.float32)
-        picked = picked.astype(jnp.bfloat16)
-        hq[:, part] = picked
-        wq_loads[c].wait()
-        queries = queries + jnp.dot(picked, wq[part, 0:qcols], preferred_element_type=jnp.float32)
-        if c == min(1, HID_CHUNKS - 1):
-            pl.semaphore_wait(barrier, n - 1 + kz - 1)
-            send_blocks(0)
-    send_queries(0, queries)
-    for h in range(1, heads):
-        rest_loads[h - 1].wait()
-        send_queries(
-            h,
-            jnp.dot(
-                hq[...], wq[:, h * qcols:(h + 1) * qcols], preferred_element_type=jnp.float32
-            ),
-        )
+
+        def go(to):
+            for index in range(len(col_parts)):
+                q_copy(h, to, index).start()
+
+        each(nq, functools.partial(sends_q, h), go)
 
     pieces = 2 if tok % (2 * LANES) == 0 else 1
     half = tok // pieces
@@ -283,51 +297,70 @@
         for h in range(1, heads):
             folded = folded + square[:, h * HEAD_DIM:(h + 1) * HEAD_DIM]
         return jnp.sum(folded.T, axis=0, keepdims=True)
-    wk_load.wait()
-    key_dev = []
+
+    def project(h):
+        return jnp.dot(
+            hq[...], wq[:, h * qcols:(h + 1) * qcols], preferred_element_type=jnp.float32
+        )
+
+    def project_chunk(c):
+        part = slice(c * step, (c + 1) * step)
+        for weight, total in ((wk, kacc), (wv, vacc)):
+            fresh = jnp.dot(hid[:, part], weight[part, :], preferred_element_type=jnp.float32)
+            total[...] = fresh if c == 0 else total[...] + fresh
+        picked = jnp.dot(pick, hid[:, part], preferred_element_type=jnp.float32)
+        hq[:, part] = picked.astype(jnp.bfloat16)
+
+    for c in range(HID_CHUNKS):
+        for copy in chunk_loads[c]:
+            copy.wait()
+        project_chunk(c)
+        if c == 0:
+            pl.semaphore_wait(barrier, n - 1 + kz - 1)
+            send_blocks(0, 0)
+            send_blocks(1, 0)
+    wq_loads[head_order[0]].wait()
+    queries = project(head_order[0])
     for p in range(pieces):
         rows = slice(p * half, (p + 1) * half)
-        fresh = jnp.dot(hid[rows, :], wk[...], preferred_element_type=jnp.float32)
-        cached = ck[rows, :].astype(jnp.float32)
-        key_dev.append(fold(fresh - cached))
+        cached_k = ck[rows, :].astype(jnp.float32)
+        cached_v = cv[rows, :].astype(jnp.float32)
         mask = jnp.concatenate([chosen_ref[rows, :]] * heads, axis=1) > 0.5
-        used = jnp.where(mask, fresh, cached).astype(jnp.bfloat16)
+        used_k = jnp.where(mask, kacc[rows, :], cached_k).astype(jnp.bfloat16)
+        used_v = jnp.where(mask, vacc[rows, :], cached_v).T.astype(jnp.bfloat16)
         for h in range(heads):
-            kall[h, axes(h)[2], core, rows, :] = used[:, h * HEAD_DIM:(h + 1) * HEAD_DIM]
-    for h in range(heads):
-        forward(0, h, axes(h)[2], core, 2).start()
-        ksend[h, cut:tok, :] = jnp.dot(
-            last_ref[...], kall[h, axes(h)[2], core], preferred_element_type=jnp.float32
-        ).astype(jnp.bfloat16)
-    wv_load.wait()
-    for p in range(pieces):
-        rows = slice(p * half, (p + 1) * half)
-        fresh = jnp.dot(hid[rows, :], wv[...], preferred_element_type=jnp.float32)
-        cached = cv[rows, :].astype(jnp.float32)
-        devbuf[zme, :, rows] = key_dev[p] + fold(fresh - cached)
-        mask = jnp.concatenate([chosen_ref[rows, :]] * heads, axis=1) > 0.5
-        used = jnp.where(mask, fresh, cached).T.astype(jnp.bfloat16)
-        for h in range(heads):
-            vall[h, axes(h)[2], core, 0:HEAD_DIM, rows] = used[h * HEAD_DIM:(h + 1) * HEAD_DIM, :]
-    for h in range(heads):
-        forward(1, h, axes(h)[2], core, 2).start()
-        vsend[h, :, cut:tok] = lax.dot_general(
-            vall[h, axes(h)[2], core, 0:HEAD_DIM, :], last_ref[...], NT,
-            preferred_element_type=jnp.float32,
-        ).astype(jnp.bfloat16)
-    send_blocks(1)
+            part = slice(h * HEAD_DIM, (h + 1) * HEAD_DIM)
+            kall[h, axes(h)[2], core, rows, :] = used_k[:, part]
+            vall[h, axes(h)[2], core, 0:HEAD_DIM, rows] = used_v[part, :]
+        devbuf[zme, :, rows] = fold(kacc[rows, :] - cached_k) + fold(vacc[rows, :] - cached_v)
+    send_queries(head_order[0], queries)
+    for h in range(heads):
+        for arr in (0, 1):
+            forward(arr, h, axes(h)[2], core, 2).start()
     sends = []
     for d in range(1, kz):
         sends.append(
             pltpu.make_async_remote_copy(
                 src_ref=devbuf.at[zme], dst_ref=devbuf.at[zme], send_sem=z_send.at[d - 1],
-                recv_sem=z_recv.at[zme], device_id={"kvh": (zme + d) % kz}, device_id_type=MESH,
+                recv_sem=z_recv.at[kz - d - 1], device_id={"kvh": (zme + d) % kz}, device_id_type=MESH,
             )
         )
         sends[-1].start()
-
-    cols = 2 * LANES if qrows % (2 * LANES) == 0 else LANES
-    col_parts = [slice(j, j + cols) for j in range(0, qrows, cols)]
+    for h in head_order[1:]:
+        wq_loads[h].wait()
+    others = [project(h) for h in head_order[1:]]
+    for h in range(heads):
+        ksend[h, cut:tok, :] = jnp.dot(
+            last_ref[...], kall[h, axes(h)[2], core], preferred_element_type=jnp.float32
+        ).astype(jnp.bfloat16)
+        vsend[h, :, cut:tok] = lax.dot_general(
+            vall[h, axes(h)[2], core, 0:HEAD_DIM, :], last_ref[...], NT,
+            preferred_element_type=jnp.float32,
+        ).astype(jnp.bfloat16)
+    send_blocks(0, 1)
+    send_blocks(1, 1)
+    for h, queries in zip(head_order[1:], others):
+        send_queries(h, queries)
 
     def run(items):
         def scores_of(item):
@@ -360,37 +393,56 @@
             acc_ref[h, q, :, part] = mixed
             scores = following
 
+    lanes = (core, 1 - core)
+
     def both(h, q, k):
-        run([(h, q, k, c, part, False) for part in col_parts for c in (core, 1 - core)])
-
-    def p_copies(h, to):
+        run([(h, q, k, c, part, False) for part in col_parts for c in lanes])
+
+    def serve(h, q, k, lanes, wait=False, answer=False):
+        for index, part in enumerate(col_parts):
+            if wait:
+                q_wait(h, q, index)
+            run([(h, q, k, c, part, False) for c in lanes])
+            if answer:
+                give_back(h, q, index)
+
+    def p_copies(h, to, index):
         qc, nq, kc, nk = axes(h)
         dest = {"seq": chip_at(h, to, kc) * 2 + core}
+        part = pl.ds(index * cols, cols)
         return [
             pltpu.make_async_remote_copy(
-                src_ref=pout.at[h, to], dst_ref=pin.at[h, qc], send_sem=p_send.at[h, to, 0],
-                recv_sem=p_recv.at[h, qc, 0], device_id=dest, device_id_type=MESH,
+                src_ref=pout.at[h, to, :, part], dst_ref=pin.at[h, qc, :, part],
+                send_sem=p_send.at[h, (to - qc - 1) % nq, index, 0],
+                recv_sem=p_recv.at[h, (qc - to - 1) % nq, index, 0],
+                device_id=dest, device_id_type=MESH,
             ),
             pltpu.make_async_remote_copy(
-                src_ref=pout_stat.at[h, to], dst_ref=pin_stat.at[h, qc],
-                send_sem=p_send.at[h, to, 1], recv_sem=p_recv.at[h, qc, 1],
+                src_ref=pout_stat.at[h, to, :, part], dst_ref=pin_stat.at[h, qc, :, part],
+                send_sem=p_send.at[h, (to - qc - 1) % nq, index, 1],
+                recv_sem=p_recv.at[h, (qc - to - 1) % nq, index, 1],
                 device_id=dest, device_id_type=MESH,
             ),
         ]
 
-    def p_wait(h, source):
+    def p_wait(h, source, index):
+        qc, nq, kc, nk = axes(h)
+        part = pl.ds(index * cols, cols)
+        place = (source - qc - 1) % nq
         for i, buf in enumerate((pin, pin_stat)):
-            view = buf.at[h, source]
+            view = buf.at[h, source, :, part]
             pltpu.make_async_remote_copy(
-                src_ref=view, dst_ref=view, send_sem=p_send.at[h, source, i],
-                recv_sem=p_recv.at[h, source, i], device_id={"seq": partner}, device_id_type=MESH,
+                src_ref=view, dst_ref=view, send_sem=p_send.at[h, place, index, i],
+                recv_sem=p_recv.at[h, place, index, i], device_id={"seq": partner},
+                device_id_type=MESH,
             ).wait_recv()
 
-    def give_back(h, to):
-        pout[h, to] = acc_ref[h, to, 0:HEAD_DIM, :].astype(jnp.bfloat16)
-        pout_stat[h, to, 0:1, :] = m_ref[h, to, 0:1, :]
-        pout_stat[h, to, 1:2, :] = acc_ref[h, to, HEAD_DIM:HEAD_DIM + 1, :]
-        for copy in p_copies(h, to):
+    def give_back(h, to, index):
+        part = col_parts[index]
+        pout[h, to, :, part] = acc_ref[h, to, 0:HEAD_DIM, part].astype(jnp.bfloat16)
+        pout_stat[h, to, 0:1, part] = m_ref[h, to, 0:1, part]
+        pout_stat[h, to, 1:2, part] = acc_ref[h, to, HEAD_DIM:HEAD_DIM + 1, part]
+        for copy in p_copies(h, to, index):
             copy.start()
 
     def no_moved(h):
@@ -403,17 +455,9 @@
             for part in col_parts
         ]
     )
-    forward_blocks(0)
     for h in range(heads):
         for arr in (0, 1):
             forward(arr, h, axes(h)[2], 1 - core, 2).wait_recv()
-    for h in range(heads):
-        def serve_own(j, h=h):
-            q_wait(h, j)
-            both(h, j, axes(h)[2])
-            pl.when(no_moved(h))(lambda: give_back(h, j))
-        each(axes(h)[1], lambda j, h=h: j > axes(h)[0], serve_own)
-    forward_blocks(1)
     @pl.when(core == 1)
     def _():
         run(
@@ -424,32 +468,63 @@
             ]
         )
     for h in range(heads):
-        def arrive(source, h=h):
-            for span in (0, 1):
-                for arr in (0, 1):
-                    forward(arr, h, source, 1 - core, span).wait_recv()
-        each(axes(h)[3], functools.partial(takes_kv, h), arrive)
-    for h in range(heads):
-        qc, nq, kc, nk = axes(h)
-
-        def serve_moved(j, h=h, qc=qc, nk=nk):
-            pl.when(j < qc)(lambda: q_wait(h, j))
-            each(nk, functools.partial(takes_kv, h), lambda i: both(h, j, i))
-            give_back(h, j)
-
-        each(
-            nq,
-            lambda j, h=h: takes_q(h, j) & jnp.logical_not(no_moved(h)),
-            serve_moved,
-        )
-    for h in range(heads):
-        qc, nq, kc, nk = axes(h)
-        each(nk, lambda i, kc=kc: i < kc, lambda i, h=h, qc=qc: both(h, qc, i))
+        forward_blocks(h, 0, functools.partial(takes_kv, h))
+        if h % 2 == 0:
+            forward_blocks(h, 1, functools.partial(takes_kv, h))
+        else:
+            forward_blocks(
+                h, 1, lambda i, h=h: takes_kv(h, i) & jnp.logical_not(shared_link(h, i))
+            )
+    def serve_own(h):
+        qc, nq, kc, nk = axes(h)
+        alone = no_moved(h)
+
+        def go(j):
+            pl.when(alone)(lambda: serve(h, j, kc, lanes, True, True))
+            pl.when(jnp.logical_not(alone))(lambda: serve(h, j, kc, lanes, True))
+
+        each(nq, lambda j: j > qc, go)
+
+    def serve_moved(h):
+        qc, nq, kc, nk = axes(h)
+
+        def wanted(j):
+            return takes_q(h, j) & jnp.logical_not(no_moved(h))
+
+        def late(j):
+            for index in range(len(col_parts)):
+                q_wait(h, j, index)
+
+        if nk == 2 and h % 2 == 1:
+            each(nq, wanted, lambda j: serve(h, j, 1 - kc, lanes[:1]))
+            arrive(h)
+            each(nq, wanted, lambda j: serve(h, j, 1 - kc, lanes[1:], False, True))
+        elif nk == 2:
+            arrive(h)
+            each(nq, lambda j: wanted(j) & (j < qc), lambda j: serve(h, j, 1 - kc, lanes, True, True))
+            each(nq, lambda j: wanted(j) & (j > qc), lambda j: serve(h, j, 1 - kc, lanes, False, True))
+        else:
+            def go(j):
+                pl.when(j < qc)(lambda: late(j))
+                each(nk, functools.partial(takes_kv, h), lambda i: both(h, j, i))
+                for index in range(len(col_parts)):
+                    give_back(h, j, index)
+
+            arrive(h)
+            each(nq, wanted, go)
+    for h in range(1, heads, 2):
+        serve_own(h)
+    for h in range(1, heads, 2):
+        forward_blocks(h, 1, lambda i, h=h: takes_kv(h, i) & shared_link(h, i))
+    for h in range(1, heads, 2):
+        serve_moved(h)
+    for h in range(0, heads, 2):
+        serve_own(h)
     for d in range(1, kz):
         src = (zme + d) % kz
         pltpu.make_async_remote_copy(
             src_ref=devbuf.at[src], dst_ref=devbuf.at[src], send_sem=z_send.at[0],
-            recv_sem=z_recv.at[src], device_id={"kvh": src}, device_id_type=MESH,
+            recv_sem=z_recv.at[d - 1], device_id={"kvh": src}, device_id_type=MESH,
         ).wait_recv()
     lens_load.wait()
     deviation = devbuf[0]
@@ -471,26 +546,34 @@
         sends.append(
             pltpu.make_async_remote_copy(
                 src_ref=docbuf.at[me], dst_ref=docbuf.at[me], send_sem=doc_send.at[d - 1],
-                recv_sem=doc_recv.at[me], device_id={"seq": (me + d) % n}, device_id_type=MESH,
+                recv_sem=doc_recv.at[n - d - 1], device_id={"seq": (me + d) % n}, device_id_type=MESH,
             )
         )
         sends[-1].start()
+    for h in range(0, heads, 2):
+        serve_moved(h)
+    for h in range(heads):
+        qc, nq, kc, nk = axes(h)
+        each(nk, lambda i, kc=kc: i < kc, lambda i, h=h, qc=qc: both(h, qc, i))
     for h in range(heads):
         qc, nq, kc, nk = axes(h)
 
         def collect(source, h=h, qc=qc):
-            p_wait(h, source)
-            best = m_ref[h, qc, 0:1, :]
-            other = pin_stat[h, source, 0:1, :]
-            top = jnp.maximum(best, other)
-            fade, rise = jnp.exp2(best - top), jnp.exp2(other - top)
-            m_ref[h, qc, 0:1, :] = top
-            acc_ref[h, qc, 0:HEAD_DIM, :] = (
-                acc_ref[h, qc, 0:HEAD_DIM, :] * fade + pin[h, source].astype(jnp.float32) * rise
-            )
-            acc_ref[h, qc, HEAD_DIM:HEAD_DIM + 1, :] = (
-                acc_ref[h, qc, HEAD_DIM:HEAD_DIM + 1, :] * fade + pin_stat[h, source, 1:2, :] * rise
-            )
+            for index, part in enumerate(col_parts):
+                p_wait(h, source, index)
+                best = m_ref[h, qc, 0:1, part]
+                other = pin_stat[h, source, 0:1, part]
+                top = jnp.maximum(best, other)
+                fade, rise = jnp.exp2(best - top), jnp.exp2(other - top)
+                m_ref[h, qc, 0:1, part] = top
+                acc_ref[h, qc, 0:HEAD_DIM, part] = (
+                    acc_ref[h, qc, 0:HEAD_DIM, part] * fade
+                    + pin[h, source, :, part].astype(jnp.float32) * rise
+                )
+                acc_ref[h, qc, HEAD_DIM:HEAD_DIM + 1, part] = (
+                    acc_ref[h, qc, HEAD_DIM:HEAD_DIM + 1, part] * fade
+                    + pin_stat[h, source, 1:2, part] * rise
+                )
 
         each(nq, functools.partial(sends_q, h), collect)
         done = acc_ref[h, qc, 0:HEAD_DIM, :] / acc_ref[h, qc, HEAD_DIM:HEAD_DIM + 1, :]
@@ -502,7 +585,7 @@
         src = (me + d) % n
         pltpu.make_async_remote_copy(
             src_ref=docbuf.at[src], dst_ref=docbuf.at[src], send_sem=doc_send.at[0],
-            recv_sem=doc_recv.at[src], device_id={"seq": src}, device_id_type=MESH,
+            recv_sem=doc_recv.at[d - 1], device_id={"seq": src}, device_id_type=MESH,
         ).wait_recv()
     totals = docbuf[0]
     for s in range(1, n):
@@ -528,14 +611,20 @@
                     forward(arr, h, source, core, span).wait_send()
 
         def drain_p(to, h=h):
-            for copy in p_copies(h, to):
-                copy.wait_send()
+            for index in range(len(col_parts)):
+                for copy in p_copies(h, to, index):
+                    copy.wait_send()
 
         for arr in (0, 1):
             forward(arr, h, kc, core, 2).wait_send()
         each(nk, functools.partial(sends_kv, h), drain_kv)
         each(nk, functools.partial(takes_kv, h), drain_forward)
-        each(nq, functools.partial(sends_q, h), lambda to, h=h: q_copy(h, to).wait_send())
+
+        def drain_q(to, h=h):
+            for index in range(len(col_parts)):
+                q_copy(h, to, index).wait_send()
+
+        each(nq, functools.partial(sends_q, h), drain_q)
         each(nq, functools.partial(takes_q, h), drain_p)
 
 
@@ -550,17 +639,18 @@
     qrows = GROUP * pad
     cut = (tok - sel_rows) // LANES * LANES
     side = max(split_chips(n // 2))
+    others = max(1, side - 1)
     bf, f32 = jnp.bfloat16, jnp.float32
     dma = pltpu.SemaphoreType.DMA
-    any_space = pl.BlockSpec(memory_space=pl.ANY)
+    hbm = pl.BlockSpec(memory_space=pltpu.HBM)
     vmem = pl.BlockSpec(memory_space=pltpu.VMEM)
     attended, score = pl.pallas_call(
         functools.partial(kernel, n, kz, docs, sel_rows),
         out_shape=(
-            jax.ShapeDtypeStruct((sel_rows, qcols), bf),
-            jax.ShapeDtypeStruct((1, tok), f32),
+            pltpu.VMEM((sel_rows, qcols), bf),
+            pltpu.VMEM((1, tok), f32),
         ),
-        in_specs=[any_space] * 8,
+        in_specs=[hbm] * 8,
         out_specs=(vmem, vmem),
         scratch_shapes=[
             pltpu.VMEM((tok, width), bf),
@@ -579,6 +669,8 @@
             pltpu.VMEM((heads, side, 2, qrows), f32),
             pltpu.VMEM((heads, side, HEAD_DIM, qrows), bf),
             pltpu.VMEM((heads, side, 2, qrows), f32),
+            pltpu.VMEM((tok, cols), f32),
+            pltpu.VMEM((tok, cols), f32),
             pltpu.VMEM((heads, side, 8, qrows), f32),
             pltpu.VMEM((heads, side, HEAD_DIM + EXTRA, qrows), f32),
             pltpu.VMEM((tok, pad), f32),
@@ -588,22 +680,24 @@
             pltpu.VMEM((n, round_up(docs, 8), 128), f32),
             pltpu.SMEM(doc_lengths.shape, jnp.int32),
             pltpu.SMEM(selected.shape, jnp.int32),
-            dma((2 * HID_CHUNKS + 5 + heads,)),
-            dma((heads, side)),
-            dma((heads, side)),
-            dma((heads, side, 2)),
-            dma((heads, side, 2)),
-            dma((heads, side, 2, 2)),
-            dma((heads, side, 2, 2)),
-            dma((heads, side, 2, 2)),
-            dma((heads, side, 2, 2)),
+            dma((3 * HID_CHUNKS + 4 + heads,)),
+            dma((heads, others, GROUP * pad // q_cols(GROUP * pad))),
+            dma((heads, others, GROUP * pad // q_cols(GROUP * pad))),
+            dma((heads, others, GROUP * pad // q_cols(GROUP * pad), 2)),
+            dma((heads, others, GROUP * pad // q_cols(GROUP * pad), 2)),
+            dma((heads, others, 2, 2)),
+            dma((heads, others, 2, 2)),
+            dma((heads, others, 2, 2)),
+            dma((heads, others, 2, 2)),
+            dma((heads, 2)),
+            dma((heads, 2)),
             dma((max(1, kz - 1),)),
-            dma((kz,)),
+            dma((max(1, kz - 1),)),
             dma((n - 1,)),
-            dma((n,)),
+            dma((n - 1,)),
         ],
         compiler_params=pltpu.CompilerParams(
-            collective_id=0, has_side_effects=True, vmem_limit_bytes=62 * 1024 * 1024
+            collective_id=0, has_side_effects=True, vmem_limit_bytes=56 * 1024 * 1024
         ),
         name="blend",
     )(hidden, w_query, w_key, w_value, cached_key, cached_value, doc_lengths, selected)

time: 32.4 us -> 27.4 us (0.85)
  Pallas kernels: 28.6 us -> 25.2 us
  local copies, waits for them, and re-layouts: 1.65 us -> 0.7 us
  other arithmetic: 1.29 us -> 0.6 us
    pallas_call x1, Pallas kernels: 28.6 us -> 25.2 us  [shards(): pl.pallas_call(functools.partial(kernel, n, kz, docs, sel_rows), out_shap...]
    unnamed x1, local copies, waits for them, and re-layouts: 1.65 us -> 0.7 us
    pallas_call x1, other arithmetic: 1.29 us -> 0.6 us  [shards(): pl.pallas_call(functools.partial(kernel, n, kz, docs, sel_rows), out_shap...]
where the time goes in v3:
time: 27.4 us; the launch traced here: 27.2 us
  Pallas kernels  25.2 us (92%)
  local copies, waits for them, and re-layouts  0.7 us (3%)
  between operations  0.64 us (2%)
  other arithmetic  0.6 us (2%)
    pallas_call x1, Pallas kernels, shards(): pl.pallas_call(functools.partial(kernel, n, kz, docs, sel_rows), out_shap...  25.2 us
    unnamed x1, local copies, waits for them, and re-layouts  0.7 us
    pallas_call x1, other arithmetic, shards(): pl.pallas_call(functools.partial(kernel, n, kz, docs, sel_rows), out_shap...  0.6 us

profile of v3, /device:TPU:0, one launch (start us, length us, event | category | flops | bytes accessed | tf_op | source)
XLA Modules:
  0.0 27.2 jit_solution(8382540846455797883)
XLA Ops:
  0.6 25.2 %blend.1 = (bf16[120,1024]{1,0:T(8,128)(2,1)S(1)}, f32[1,768]{1,0:T(1,128)S(1)}) custom-call(bf16[768,4096]{1,0:T(8,128)(2,1)} %hid_hbm.1, bf16[4096,1024]{1,0:T(8,128)(2,1)} %wq_hbm.1, bf16[4096,256]{1,0:T(8,128)(2,1)} %wk_hbm.1, bf16[4096,256]{1,0:T(8,128)(2,1)} %wv_hbm.1, bf16[768,256]{1,0:T(8,128)(2,1)} %ck_hbm.1, bf16[768,256]{1,0:T(8,128)(2,1)} %cv_hbm.1, ...), custom_call_target="tpu_custom_call" | custom-call | tf_op jit(solution)/shard_map/blend/pallas_call | solution.py:647
  25.9 0.7 %copy.11 = bf16[120,1024]{1,0:T(8,128)(2,1)} copy(bf16[120,1024]{1,0:T(8,128)(2,1)S(1)} %get-tuple-element.6) | data formatting | bytes 491520
  26.6 0.6 %reduce = f32[768]{0:T(1024)} reduce(f32[1,768]{1,0:T(1,128)S(1)} %get-tuple-element.5, f32[]{:T(128)} %constant), dimensions={0}, to_apply=%get-tuple-element.5.reduce_sub_computation | reduce | bytes 6148 | tf_op jit(solution)/shard_map/blend/pallas_call | solution.py:647

commit v4 on v3

--- a/solution.py
+++ b/solution.py
@@ -124,11 +124,20 @@
             return (source != qc) & ((source > qc) | (kc > 0))
         return source > qc
 
-    def each(count, want, body):
+    def each(mine, count, want, body):
         def go(i, carry):
             pl.when(want(i))(functools.partial(body, i))
             return carry
-        lax.fori_loop(0, count, go, 0)
+        if count == 2:
+            go(1 - mine, 0)
+        else:
+            lax.fori_loop(0, count, go, 0)
+
+    def each_q(h, want, body):
+        each(axes(h)[0], axes(h)[1], want, body)
+
+    def each_k(h, want, body):
+        each(axes(h)[2], axes(h)[3], want, body)
 
     def block(arr, h, slot, which, span):
         first, rows = spans[span]
@@ -174,7 +183,7 @@
         for h in range(heads):
             def go(to, h=h):
                 move(arr, h, span, to).start()
-            each(axes(h)[3], functools.partial(sends_kv, h), go)
+            each_k(h, functools.partial(sends_kv, h), go)
 
     def shared_link(h, source):
         qc, nq, kc, nk = axes(h)
@@ -185,14 +194,14 @@
             for arr in (0, 1):
                 moved(arr, h, span, source).wait_recv()
                 forward(arr, h, source, core, span).start()
-        each(axes(h)[3], want, go)
+        each_k(h, want, go)
 
     def arrive(h):
         def go(source):
             for span in (0, 1):
                 for arr in (0, 1):
                     forward(arr, h, source, 1 - core, span).wait_recv()
-        each(axes(h)[3], functools.partial(takes_kv, h), go)
+        each_k(h, functools.partial(takes_kv, h), go)
 
     for h in range(heads):
         for i in range(kall.shape[1]):
@@ -276,17 +285,19 @@
             recv_sem=q_recv.at[h, place, index], device_id={"seq": partner}, device_id_type=MESH,
         ).wait_recv()
 
-    def send_queries(h, queries):
-        qc, nq, kc, nk = axes(h)
+    def store_queries(h, queries):
         scaled = (queries * EXP_SCALE).astype(jnp.bfloat16)
         for g in range(GROUP):
-            qbuf[h, qc, g * pad:(g + 1) * pad, :] = scaled[:, g * HEAD_DIM:(g + 1) * HEAD_DIM]
-
+            qbuf[h, axes(h)[0], g * pad:(g + 1) * pad, :] = scaled[
+                :, g * HEAD_DIM:(g + 1) * HEAD_DIM
+            ]
+
+    def send_queries(h):
         def go(to):
             for index in range(len(col_parts)):
                 q_copy(h, to, index).start()
 
-        each(nq, functools.partial(sends_q, h), go)
+        each_q(h, functools.partial(sends_q, h), go)
 
     pieces = 2 if tok % (2 * LANES) == 0 else 1
     half = tok // pieces
@@ -319,36 +330,36 @@
             pl.semaphore_wait(barrier, n - 1 + kz - 1)
             send_blocks(0, 0)
             send_blocks(1, 0)
-    wq_loads[head_order[0]].wait()
-    queries = project(head_order[0])
+
+    first, rest = head_order[0], head_order[1:]
+    wq_loads[first].wait()
+    queries = project(first)
+    mask = [
+        jnp.concatenate([chosen_ref[p * half:(p + 1) * half, :]] * heads, axis=1) > 0.5
+        for p in range(pieces)
+    ]
+    for p in range(pieces):
+        rows = slice(p * half, (p + 1) * half)
+        cached = ck[rows, :].astype(jnp.float32)
+        used = jnp.where(mask[p], kacc[rows, :], cached).astype(jnp.bfloat16)
+        for h in range(heads):
+            kall[h, axes(h)[2], core, rows, :] = used[:, h * HEAD_DIM:(h + 1) * HEAD_DIM]
+    store_queries(first, queries)
+    send_queries(first)
+    for h in range(heads):
+        forward(0, h, axes(h)[2], core, 2).start()
+    for h in rest:
+        wq_loads[h].wait()
+    queries = {h: project(h) for h in rest}
     for p in range(pieces):
         rows = slice(p * half, (p + 1) * half)
         cached_k = ck[rows, :].astype(jnp.float32)
         cached_v = cv[rows, :].astype(jnp.float32)
-        mask = jnp.concatenate([chosen_ref[rows, :]] * heads, axis=1) > 0.5
-        used_k = jnp.where(mask, kacc[rows, :], cached_k).astype(jnp.bfloat16)
-        used_v = jnp.where(mask, vacc[rows, :], cached_v).T.astype(jnp.bfloat16)
+        used = jnp.where(mask[p], vacc[rows, :], cached_v).T.astype(jnp.bfloat16)
         for h in range(heads):
             part = slice(h * HEAD_DIM, (h + 1) * HEAD_DIM)
-            kall[h, axes(h)[2], core, rows, :] = used_k[:, part]
-            vall[h, axes(h)[2], core, 0:HEAD_DIM, rows] = used_v[part, :]
+            vall[h, axes(h)[2], core, 0:HEAD_DIM, rows] = used[part, :]
         devbuf[zme, :, rows] = fold(kacc[rows, :] - cached_k) + fold(vacc[rows, :] - cached_v)
-    send_queries(head_order[0], queries)
-    for h in range(heads):
-        for arr in (0, 1):
-            forward(arr, h, axes(h)[2], core, 2).start()
-    sends = []
-    for d in range(1, kz):
-        sends.append(
-            pltpu.make_async_remote_copy(
-                src_ref=devbuf.at[zme], dst_ref=devbuf.at[zme], send_sem=z_send.at[d - 1],
-                recv_sem=z_recv.at[kz - d - 1], device_id={"kvh": (zme + d) % kz}, device_id_type=MESH,
-            )
-        )
-        sends[-1].start()
-    for h in head_order[1:]:
-        wq_loads[h].wait()
-    others = [project(h) for h in head_order[1:]]
     for h in range(heads):
         ksend[h, cut:tok, :] = jnp.dot(
             last_ref[...], kall[h, axes(h)[2], core], preferred_element_type=jnp.float32
@@ -357,24 +368,33 @@
             vall[h, axes(h)[2], core, 0:HEAD_DIM, :], last_ref[...], NT,
             preferred_element_type=jnp.float32,
         ).astype(jnp.bfloat16)
+    for h in rest:
+        store_queries(h, queries[h])
+    for h in range(heads):
+        forward(1, h, axes(h)[2], core, 2).start()
     send_blocks(0, 1)
     send_blocks(1, 1)
-    for h, queries in zip(head_order[1:], others):
-        send_queries(h, queries)
-
-    def run(items):
+    for h in rest:
+        send_queries(h)
+    sends = []
+    for d in range(1, kz):
+        sends.append(
+            pltpu.make_async_remote_copy(
+                src_ref=devbuf.at[zme], dst_ref=devbuf.at[zme], send_sem=z_send.at[d - 1],
+                recv_sem=z_recv.at[kz - d - 1], device_id={"kvh": (zme + d) % kz},
+                device_id_type=MESH,
+            )
+        )
+        sends[-1].start()
+
+    def run(items, answers=()):
         def scores_of(item):
             h, q, k, which, part, masked = item
             s = lax.dot_general(
                 kall[h, k, which], qbuf[h, q, part, :], NT, preferred_element_type=jnp.float32
             )
             if masked:
-                first = part.start % pad
-                if cols <= pad:
-                    bias = bias_ref[:, first:first + cols]
-                else:
-                    bias = jnp.concatenate([bias_ref[...]] * (cols // pad), axis=1)
-                s = s + bias
+                s = s + jnp.concatenate([bias_ref[...]] * GROUP, axis=1)
             return s
 
         scores = scores_of(items[0])
@@ -392,33 +412,38 @@
             m_ref[h, q, 0:1, part] = best
             acc_ref[h, q, :, part] = mixed
             scores = following
+            if answers and (i + 1) % (len(items) // len(answers)) == 0:
+                give_back(h, q, answers[i * len(answers) // len(items)])
 
     lanes = (core, 1 - core)
+    wide = slice(0, qrows)
 
     def both(h, q, k):
-        run([(h, q, k, c, part, False) for part in col_parts for c in lanes])
-
-    def serve(h, q, k, lanes, wait=False, answer=False):
-        for index, part in enumerate(col_parts):
-            if wait:
+        run([(h, q, k, c, wide, False) for c in lanes])
+
+    every = range(len(col_parts))
+
+    def serve(h, q, k, lanes, wait=False, answer=False, indices=every):
+        items = {x: [(h, q, k, c, col_parts[x], False) for c in lanes] for x in indices}
+        if wait:
+            for index in indices:
                 q_wait(h, q, index)
-            run([(h, q, k, c, part, False) for c in lanes])
-            if answer:
-                give_back(h, q, index)
+                run(items[index], [index] if answer else ())
+            return
+        run(sum(items.values(), []), indices if answer else ())
 
     def p_copies(h, to, index):
         qc, nq, kc, nk = axes(h)
         dest = {"seq": chip_at(h, to, kc) * 2 + core}
-        part = pl.ds(index * cols, cols)
         return [
             pltpu.make_async_remote_copy(
-                src_ref=pout.at[h, to, :, part], dst_ref=pin.at[h, qc, :, part],
+                src_ref=pout.at[h, to, index], dst_ref=pin.at[h, qc, index],
                 send_sem=p_send.at[h, (to - qc - 1) % nq, index, 0],
                 recv_sem=p_recv.at[h, (qc - to - 1) % nq, index, 0],
                 device_id=dest, device_id_type=MESH,
             ),
             pltpu.make_async_remote_copy(
-                src_ref=pout_stat.at[h, to, :, part], dst_ref=pin_stat.at[h, qc, :, part],
+                src_ref=pout_stat.at[h, to, index], dst_ref=pin_stat.at[h, qc, index],
                 send_sem=p_send.at[h, (to - qc - 1) % nq, index, 1],
                 recv_sem=p_recv.at[h, (qc - to - 1) % nq, index, 1],
                 device_id=dest, device_id_type=MESH,
@@ -427,10 +452,9 @@
 
     def p_wait(h, source, index):
         qc, nq, kc, nk = axes(h)
-        part = pl.ds(index * cols, cols)
         place = (source - qc - 1) % nq
         for i, buf in enumerate((pin, pin_stat)):
-            view = buf.at[h, source, :, part]
+            view = buf.at[h, source, index]
             pltpu.make_async_remote_copy(
                 src_ref=view, dst_ref=view, send_sem=p_send.at[h, place, index, i],
                 recv_sem=p_recv.at[h, place, index, i], device_id={"seq": partner},
@@ -439,9 +463,9 @@
 
     def give_back(h, to, index):
         part = col_parts[index]
-        pout[h, to, :, part] = acc_ref[h, to, 0:HEAD_DIM, part].astype(jnp.bfloat16)
-        pout_stat[h, to, 0:1, part] = m_ref[h, to, 0:1, part]
-        pout_stat[h, to, 1:2, part] = acc_ref[h, to, HEAD_DIM:HEAD_DIM + 1, part]
+        pout[h, to, index] = acc_ref[h, to, 0:HEAD_DIM, part].astype(jnp.bfloat16)
+        pout_stat[h, to, index, 0:1, :] = m_ref[h, to, 0:1, part]
+        pout_stat[h, to, index, 1:2, :] = acc_ref[h, to, HEAD_DIM:HEAD_DIM + 1, part]
         for copy in p_copies(h, to, index):
             copy.start()
 
@@ -450,9 +474,8 @@
         return kc == 0 if h % 2 == 0 else nk == 1
     run(
         [
-            (h, axes(h)[0], axes(h)[2], core, part, True)
+            (h, axes(h)[0], axes(h)[2], core, wide, True)
             for h in range(heads)
-            for part in col_parts
         ]
     )
     for h in range(heads):
@@ -462,11 +485,75 @@
     def _():
         run(
             [
-                (h, axes(h)[0], axes(h)[2], 0, part, False)
+                (h, axes(h)[0], axes(h)[2], 0, wide, False)
                 for h in range(heads)
-                for part in col_parts
             ]
         )
+
+    def serve_own(h, indices=every):
+        qc, nq, kc, nk = axes(h)
+        alone = no_moved(h)
+
+        def go(j):
+            pl.when(alone)(lambda: serve(h, j, kc, lanes, True, True, indices))
+            if indices[-1] == every[-1]:
+                pl.when(jnp.logical_not(alone))(lambda: serve(h, j, kc, lanes, True))
+
+        each_q(h, lambda j: j > qc, go)
+
+    def moved_wanted(h, j):
+        return takes_q(h, j) & jnp.logical_not(no_moved(h))
+
+    def near_lane(h):
+        qc, nq, kc, nk = axes(h)
+        if nk == 2:
+            each_q(
+                h, functools.partial(moved_wanted, h), lambda j: serve(h, j, 1 - kc, lanes[:1])
+            )
+
+    def far_lane(h):
+        qc, nq, kc, nk = axes(h)
+
+        def go(j):
+            each_k(h, functools.partial(takes_kv, h), lambda i: both(h, j, i))
+            for index in every:
+                give_back(h, j, index)
+
+        arrive(h)
+        if nk == 2:
+            each_q(
+                h, functools.partial(moved_wanted, h),
+                lambda j: serve(h, j, 1 - kc, lanes[1:], False, True),
+            )
+        else:
+            each_q(h, functools.partial(moved_wanted, h), go)
+
+    def serve_moved(h):
+        qc, nq, kc, nk = axes(h)
+
+        def go(j):
+            @pl.when(j < qc)
+            def _():
+                for index in every:
+                    q_wait(h, j, index)
+            each_k(h, functools.partial(takes_kv, h), lambda i: both(h, j, i))
+            for index in every:
+                give_back(h, j, index)
+
+        arrive(h)
+        if nk == 2:
+            each_q(
+                h, lambda j: moved_wanted(h, j) & (j < qc),
+                lambda j: serve(h, j, 1 - kc, lanes, True, True),
+            )
+            each_q(
+                h, lambda j: moved_wanted(h, j) & (j > qc),
+                lambda j: serve(h, j, 1 - kc, lanes, False, True),
+            )
+        else:
+            each_q(h, functools.partial(moved_wanted, h), go)
+    for h in range(1, heads, 2):
+        serve_own(h)
     for h in range(heads):
         forward_blocks(h, 0, functools.partial(takes_kv, h))
         if h % 2 == 0:
@@ -475,51 +562,6 @@
             forward_blocks(
                 h, 1, lambda i, h=h: takes_kv(h, i) & jnp.logical_not(shared_link(h, i))
             )
-    def serve_own(h):
-        qc, nq, kc, nk = axes(h)
-        alone = no_moved(h)
-
-        def go(j):
-            pl.when(alone)(lambda: serve(h, j, kc, lanes, True, True))
-            pl.when(jnp.logical_not(alone))(lambda: serve(h, j, kc, lanes, True))
-
-        each(nq, lambda j: j > qc, go)
-
-    def serve_moved(h):
-        qc, nq, kc, nk = axes(h)
-
-        def wanted(j):
-            return takes_q(h, j) & jnp.logical_not(no_moved(h))
-
-        def late(j):
-            for index in range(len(col_parts)):
-                q_wait(h, j, index)
-
-        if nk == 2 and h % 2 == 1:
-            each(nq, wanted, lambda j: serve(h, j, 1 - kc, lanes[:1]))
-            arrive(h)
-            each(nq, wanted, lambda j: serve(h, j, 1 - kc, lanes[1:], False, True))
-        elif nk == 2:
-            arrive(h)
-            each(nq, lambda j: wanted(j) & (j < qc), lambda j: serve(h, j, 1 - kc, lanes, True, True))
-            each(nq, lambda j: wanted(j) & (j > qc), lambda j: serve(h, j, 1 - kc, lanes, False, True))
-        else:
-            def go(j):
-                pl.when(j < qc)(lambda: late(j))
-                each(nk, functools.partial(takes_kv, h), lambda i: both(h, j, i))
-                for index in range(len(col_parts)):
-                    give_back(h, j, index)
-
-            arrive(h)
-            each(nq, wanted, go)
-    for h in range(1, heads, 2):
-        serve_own(h)
-    for h in range(1, heads, 2):
-        forward_blocks(h, 1, lambda i, h=h: takes_kv(h, i) & shared_link(h, i))
-    for h in range(1, heads, 2):
-        serve_moved(h)
-    for h in range(0, heads, 2):
-        serve_own(h)
     for d in range(1, kz):
         src = (zme + d) % kz
         pltpu.make_async_remote_copy(
@@ -550,11 +592,21 @@
             )
         )
         sends[-1].start()
+    for h in range(1, heads, 2):
+        forward_blocks(h, 1, lambda i, h=h: takes_kv(h, i) & shared_link(h, i))
+    for h in range(1, heads, 2):
+        near_lane(h)
+    for h in range(0, heads, 2):
+        serve_own(h, every[:1])
+    for h in range(1, heads, 2):
+        far_lane(h)
+    for h in range(0, heads, 2):
+        serve_own(h, every[1:])
     for h in range(0, heads, 2):
         serve_moved(h)
     for h in range(heads):
         qc, nq, kc, nk = axes(h)
-        each(nk, lambda i, kc=kc: i < kc, lambda i, h=h, qc=qc: both(h, qc, i))
+        each_k(h, lambda i, kc=kc: i < kc, lambda i, h=h, qc=qc: both(h, qc, i))
     for h in range(heads):
         qc, nq, kc, nk = axes(h)
 
@@ -562,20 +614,20 @@
             for index, part in enumerate(col_parts):
                 p_wait(h, source, index)
                 best = m_ref[h, qc, 0:1, part]
-                other = pin_stat[h, source, 0:1, part]
+                other = pin_stat[h, source, index, 0:1, :]
                 top = jnp.maximum(best, other)
                 fade, rise = jnp.exp2(best - top), jnp.exp2(other - top)
                 m_ref[h, qc, 0:1, part] = top
                 acc_ref[h, qc, 0:HEAD_DIM, part] = (
                     acc_ref[h, qc, 0:HEAD_DIM, part] * fade
-                    + pin[h, source, :, part].astype(jnp.float32) * rise
+                    + pin[h, source, index].astype(jnp.float32) * rise
                 )
                 acc_ref[h, qc, HEAD_DIM:HEAD_DIM + 1, part] = (
                     acc_ref[h, qc, HEAD_DIM:HEAD_DIM + 1, part] * fade
-                    + pin_stat[h, source, 1:2, part] * rise
+                    + pin_stat[h, source, index, 1:2, :] * rise
                 )
 
-        each(nq, functools.partial(sends_q, h), collect)
+        each_q(h, functools.partial(sends_q, h), collect)
         done = acc_ref[h, qc, 0:HEAD_DIM, :] / acc_ref[h, qc, HEAD_DIM:HEAD_DIM + 1, :]
         for g in range(GROUP):
             head = h * GROUP + g
@@ -617,15 +669,15 @@
 
         for arr in (0, 1):
             forward(arr, h, kc, core, 2).wait_send()
-        each(nk, functools.partial(sends_kv, h), drain_kv)
-        each(nk, functools.partial(takes_kv, h), drain_forward)
+        each_k(h, functools.partial(sends_kv, h), drain_kv)
+        each_k(h, functools.partial(takes_kv, h), drain_forward)
 
         def drain_q(to, h=h):
             for index in range(len(col_parts)):
                 q_copy(h, to, index).wait_send()
 
-        each(nq, functools.partial(sends_q, h), drain_q)
-        each(nq, functools.partial(takes_q, h), drain_p)
+        each_q(h, functools.partial(sends_q, h), drain_q)
+        each_q(h, functools.partial(takes_q, h), drain_p)
 
 
 def shards(n, kz, hidden, w_query, w_key, w_value, cached_key, cached_value, doc_lengths, selected):
@@ -638,6 +690,7 @@
     heads = cols // HEAD_DIM
     qrows = GROUP * pad
     cut = (tok - sel_rows) // LANES * LANES
+    cut_q = q_cols(qrows)
     side = max(split_chips(n // 2))
     others = max(1, side - 1)
     bf, f32 = jnp.bfloat16, jnp.float32
@@ -665,10 +718,10 @@
             pltpu.VMEM((heads, tok, HEAD_DIM), bf),
             pltpu.VMEM((heads, HEAD_DIM, tok), bf),
             pltpu.VMEM((heads, side, qrows, HEAD_DIM), bf),
-            pltpu.VMEM((heads, side, HEAD_DIM, qrows), bf),
-            pltpu.VMEM((heads, side, 2, qrows), f32),
-            pltpu.VMEM((heads, side, HEAD_DIM, qrows), bf),
-            pltpu.VMEM((heads, side, 2, qrows), f32),
+            pltpu.VMEM((heads, side, qrows // cut_q, HEAD_DIM, cut_q), bf),
+            pltpu.VMEM((heads, side, qrows // cut_q, 2, cut_q), f32),
+            pltpu.VMEM((heads, side, qrows // cut_q, HEAD_DIM, cut_q), bf),
+            pltpu.VMEM((heads, side, qrows // cut_q, 2, cut_q), f32),
             pltpu.VMEM((tok, cols), f32),
             pltpu.VMEM((tok, cols), f32),
             pltpu.VMEM((heads, side, 8, qrows), f32),
@@ -681,10 +734,10 @@
             pltpu.SMEM(doc_lengths.shape, jnp.int32),
             pltpu.SMEM(selected.shape, jnp.int32),
             dma((3 * HID_CHUNKS + 4 + heads,)),
-            dma((heads, others, GROUP * pad // q_cols(GROUP * pad))),
-            dma((heads, others, GROUP * pad // q_cols(GROUP * pad))),
-            dma((heads, others, GROUP * pad // q_cols(GROUP * pad), 2)),
-            dma((heads, others, GROUP * pad // q_cols(GROUP * pad), 2)),
+            dma((heads, others, qrows // cut_q)),
+            dma((heads, others, qrows // cut_q)),
+            dma((heads, others, qrows // cut_q, 2)),
+            dma((heads, others, qrows // cut_q, 2)),
             dma((heads, others, 2, 2)),
             dma((heads, others, 2, 2)),
             dma((heads, others, 2, 2)),

time: 27.4 us -> 25.5 us (0.931)
  Pallas kernels: 25.2 us -> 23.4 us
    pallas_call x1, Pallas kernels: 25.2 us -> 23.4 us  [shards(): pl.pallas_call(functools.partial(kernel, n, kz, docs, sel_rows), out_shap...]
where the time goes in v4:
time: 25.5 us; the launch traced here: 25.3 us
  Pallas kernels  23.4 us (92%)
  local copies, waits for them, and re-layouts  0.7 us (3%)
  between operations  0.64 us (3%)
  other arithmetic  0.6 us (2%)
    pallas_call x1, Pallas kernels, shards(): pl.pallas_call(functools.partial(kernel, n, kz, docs, sel_rows), out_shap...  23.4 us
    unnamed x1, local copies, waits for them, and re-layouts  0.7 us
    pallas_call x1, other arithmetic, shards(): pl.pallas_call(functools.partial(kernel, n, kz, docs, sel_rows), out_shap...  0.6 us

profile of v4, /device:TPU:0, one launch (start us, length us, event | category | flops | bytes accessed | tf_op | source)
XLA Modules:
  0.0 25.3 jit_solution(18074775915586237067)
XLA Ops:
  0.6 23.4 %blend.1 = (bf16[120,1024]{1,0:T(8,128)(2,1)S(1)}, f32[1,768]{1,0:T(1,128)S(1)}) custom-call(bf16[768,4096]{1,0:T(8,128)(2,1)} %hid_hbm.1, bf16[4096,1024]{1,0:T(8,128)(2,1)} %wq_hbm.1, bf16[4096,256]{1,0:T(8,128)(2,1)} %wk_hbm.1, bf16[4096,256]{1,0:T(8,128)(2,1)} %wv_hbm.1, bf16[768,256]{1,0:T(8,128)(2,1)} %ck_hbm.1, bf16[768,256]{1,0:T(8,128)(2,1)} %cv_hbm.1, ...), custom_call_target="tpu_custom_call" | custom-call | tf_op jit(solution)/shard_map/blend/pallas_call | solution.py:700
  24.0 0.7 %copy.11 = bf16[120,1024]{1,0:T(8,128)(2,1)} copy(bf16[120,1024]{1,0:T(8,128)(2,1)S(1)} %get-tuple-element.6) | data formatting | bytes 491520
  24.7 0.6 %reduce = f32[768]{0:T(1024)} reduce(f32[1,768]{1,0:T(1,128)S(1)} %get-tuple-element.5, f32[]{:T(128)} %constant), dimensions={0}, to_apply=%get-tuple-element.5.reduce_sub_computation | reduce | bytes 6148 | tf_op jit(solution)/shard_map/blend/pallas_call | solution.py:700

commit v5 on v4

--- a/solution.py
+++ b/solution.py
@@ -40,7 +40,7 @@
     hid, wq, wk, wv, ck, cv, hq, kall, vall, ksend, vsend, qbuf, pout, pout_stat, pin, pin_stat,
     kacc, vacc, m_ref, acc_ref, bias_ref, chosen_ref, last_ref, devbuf, docbuf, lens_ref, sel_ref,
     load_sem, q_send, q_recv, p_send, p_recv, mv_send, mv_recv, fw_send, fw_recv, own_send, own_recv,
-    z_send, z_recv, doc_send, doc_recv,
+    z_send, z_recv, doc_send, doc_recv, ready,
 ):
     tok, width = hid.shape
     heads = wk.shape[1] // HEAD_DIM
@@ -59,10 +59,26 @@
     partner = me + 1 - 2 * core
     step = width // HID_CHUNKS
     barrier = pltpu.get_barrier_semaphore()
-    for d in range(1, n):
-        pl.semaphore_signal(barrier, inc=1, device_id={"seq": (me + d) % n}, device_id_type=MESH)
+    for c in range(n // 2):
+        @pl.when(me != 2 * c + 1)
+        def _():
+            pl.semaphore_signal(
+                barrier, inc=1, device_id={"seq": 2 * c + 1}, device_id_type=MESH
+            )
     for d in range(1, kz):
-        pl.semaphore_signal(barrier, inc=1, device_id={"kvh": (zme + d) % kz}, device_id_type=MESH)
+        pl.semaphore_signal(
+            barrier, inc=1, device_id={"seq": 2 * chip, "kvh": (zme + d) % kz},
+            device_id_type=MESH,
+        )
+
+    def tell(hearing, count):
+        @pl.when(core == hearing)
+        def _():
+            pl.semaphore_wait(barrier, count)
+            pl.semaphore_signal(ready, inc=1, device_id={"seq": partner}, device_id_type=MESH)
+
+    def hear(hearing):
+        pl.when(core != hearing)(lambda: pl.semaphore_wait(ready, 1))
 
     loads = []
 
@@ -179,11 +195,16 @@
             device_id={"seq": partner}, device_id_type=MESH,
         )
 
-    def send_blocks(arr, span):
+    def urgent(h):
+        return True if h % 2 == 0 else ia < rows_a - 1
+
+    def send_blocks(arr, span, want=lambda h: True, only=range(2)):
         for h in range(heads):
+            if h % 2 not in only:
+                continue
             def go(to, h=h):
                 move(arr, h, span, to).start()
-            each_k(h, functools.partial(sends_kv, h), go)
+            each_k(h, lambda to, h=h: sends_kv(h, to) & want(h), go)
 
     def shared_link(h, source):
         qc, nq, kc, nk = axes(h)
@@ -321,16 +342,16 @@
             total[...] = fresh if c == 0 else total[...] + fresh
         picked = jnp.dot(pick, hid[:, part], preferred_element_type=jnp.float32)
         hq[:, part] = picked.astype(jnp.bfloat16)
-
+    tell(1, n - 1)
+    hear(1)
+    send_blocks(0, 0)
+    send_blocks(1, 0)
     for c in range(HID_CHUNKS):
         for copy in chunk_loads[c]:
             copy.wait()
         project_chunk(c)
-        if c == 0:
-            pl.semaphore_wait(barrier, n - 1 + kz - 1)
-            send_blocks(0, 0)
-            send_blocks(1, 0)
-
+    if kz > 1:
+        tell(0, 2 * (kz - 1))
     first, rest = head_order[0], head_order[1:]
     wq_loads[first].wait()
     queries = project(first)
@@ -372,11 +393,15 @@
         store_queries(h, queries[h])
     for h in range(heads):
         forward(1, h, axes(h)[2], core, 2).start()
-    send_blocks(0, 1)
-    send_blocks(1, 1)
+    send_blocks(0, 1, urgent)
+    send_blocks(1, 1, urgent)
     for h in rest:
         send_queries(h)
+    for arr in (0, 1):
+        send_blocks(arr, 1, lambda h: jnp.logical_not(urgent(h)), (1,))
     sends = []
+    if kz > 1:
+        hear(0)
     for d in range(1, kz):
         sends.append(
             pltpu.make_async_remote_copy(
@@ -519,7 +544,7 @@
             for index in every:
                 give_back(h, j, index)
 
-        arrive(h)
+        pl.when(ia < rows_a - 1)(lambda: arrive(h))
         if nk == 2:
             each_q(
                 h, functools.partial(moved_wanted, h),
@@ -593,7 +618,9 @@
         )
         sends[-1].start()
     for h in range(1, heads, 2):
-        forward_blocks(h, 1, lambda i, h=h: takes_kv(h, i) & shared_link(h, i))
+        forward_blocks(
+            h, 1, lambda i, h=h: takes_kv(h, i) & shared_link(h, i) & (ia < rows_a - 1)
+        )
     for h in range(1, heads, 2):
         near_lane(h)
     for h in range(0, heads, 2):
@@ -606,6 +633,11 @@
         serve_moved(h)
     for h in range(heads):
         qc, nq, kc, nk = axes(h)
+        if h % 2 == 1:
+            @pl.when(ia == rows_a - 1)
+            def _():
+                forward_blocks(h, 1, functools.partial(takes_kv, h))
+                arrive(h)
         each_k(h, lambda i, kc=kc: i < kc, lambda i, h=h, qc=qc: both(h, qc, i))
     for h in range(heads):
         qc, nq, kc, nk = axes(h)
@@ -748,6 +780,7 @@
             dma((max(1, kz - 1),)),
             dma((n - 1,)),
             dma((n - 1,)),
+            pltpu.SemaphoreType.REGULAR,
         ],
         compiler_params=pltpu.CompilerParams(
             collective_id=0, has_side_effects=True, vmem_limit_bytes=56 * 1024 * 1024

time: 25.5 us -> 24.6 us (0.965)
  Pallas kernels: 23.4 us -> 22.5 us
    pallas_call x1, Pallas kernels: 23.4 us -> 22.5 us  [shards(): pl.pallas_call(functools.partial(kernel, n, kz, docs, sel_rows), out_shap...]
where the time goes in v5:
time: 24.6 us; the launch traced here: 24.5 us
  Pallas kernels  22.5 us (91%)
  local copies, waits for them, and re-layouts  0.7 us (3%)
  between operations  0.64 us (3%)
  other arithmetic  0.6 us (2%)
    pallas_call x1, Pallas kernels, shards(): pl.pallas_call(functools.partial(kernel, n, kz, docs, sel_rows), out_shap...  22.5 us
    unnamed x1, local copies, waits for them, and re-layouts  0.7 us
    pallas_call x1, other arithmetic, shards(): pl.pallas_call(functools.partial(kernel, n, kz, docs, sel_rows), out_shap...  0.6 us

profile of v5, /device:TPU:0, one launch (start us, length us, event | category | flops | bytes accessed | tf_op | source)
XLA Modules:
  0.0 24.5 jit_solution(3733515182547851441)
XLA Ops:
  0.6 22.5 %blend.1 = (bf16[120,1024]{1,0:T(8,128)(2,1)S(1)}, f32[1,768]{1,0:T(1,128)S(1)}) custom-call(bf16[768,4096]{1,0:T(8,128)(2,1)} %hid_hbm.1, bf16[4096,1024]{1,0:T(8,128)(2,1)} %wq_hbm.1, bf16[4096,256]{1,0:T(8,128)(2,1)} %wk_hbm.1, bf16[4096,256]{1,0:T(8,128)(2,1)} %wv_hbm.1, bf16[768,256]{1,0:T(8,128)(2,1)} %ck_hbm.1, bf16[768,256]{1,0:T(8,128)(2,1)} %cv_hbm.1, ...), custom_call_target="tpu_custom_call" | custom-call | tf_op jit(solution)/shard_map/blend/pallas_call | solution.py:732
  23.2 0.7 %copy.11 = bf16[120,1024]{1,0:T(8,128)(2,1)} copy(bf16[120,1024]{1,0:T(8,128)(2,1)S(1)} %get-tuple-element.6) | data formatting | bytes 491520
  23.9 0.6 %reduce = f32[768]{0:T(1024)} reduce(f32[1,768]{1,0:T(1,128)S(1)} %get-tuple-element.5, f32[]{:T(128)} %constant), dimensions={0}, to_apply=%get-tuple-element.5.reduce_sub_computation | reduce | bytes 6148 | tf_op jit(solution)/shard_map/blend/pallas_call | solution.py:732

commit v6 on v5

--- a/solution.py
+++ b/solution.py
@@ -38,7 +38,7 @@
     hid_hbm, wq_hbm, wk_hbm, wv_hbm, ck_hbm, cv_hbm, lens_hbm, sel_hbm,
     out_ref, score_ref,
     hid, wq, wk, wv, ck, cv, hq, kall, vall, ksend, vsend, qbuf, pout, pout_stat, pin, pin_stat,
-    kacc, vacc, m_ref, acc_ref, bias_ref, chosen_ref, last_ref, devbuf, docbuf, lens_ref, sel_ref,
+    kacc, vacc, m_ref, acc_ref, bias_ref, chosen_ref, last_ref, dev_ref, devbuf, docbuf, lens_ref, sel_ref,
     load_sem, q_send, q_recv, p_send, p_recv, mv_send, mv_recv, fw_send, fw_recv, own_send, own_recv,
     z_send, z_recv, doc_send, doc_recv, ready,
 ):
@@ -515,14 +515,27 @@
             ]
         )
 
-    def serve_own(h, indices=every):
+    def serve_own(h, early):
         qc, nq, kc, nk = axes(h)
         alone = no_moved(h)
 
+        def part(j, index):
+            serve(h, j, kc, lanes, True, False, (index,))
+
+        def answer(j, index):
+            pl.when(alone)(lambda: give_back(h, j, index))
+
         def go(j):
-            pl.when(alone)(lambda: serve(h, j, kc, lanes, True, True, indices))
-            if indices[-1] == every[-1]:
-                pl.when(jnp.logical_not(alone))(lambda: serve(h, j, kc, lanes, True))
+            if early:
+                @pl.when(alone)
+                def _():
+                    part(j, 0)
+                    give_back(h, j, 0)
+                return
+            pl.when(jnp.logical_not(alone))(lambda: part(j, 0))
+            for index in every[1:]:
+                part(j, index)
+                answer(j, index)
 
         each_q(h, lambda j: j > qc, go)
 
@@ -553,6 +566,13 @@
         else:
             each_q(h, functools.partial(moved_wanted, h), go)
 
+    def earlier(h, j):
+        other = 1 - axes(h)[2]
+        serve(h, j, other, lanes, True, True, every[:1])
+        if h == 0 and halved:
+            pl.when(corner)(exchange)
+        serve(h, j, other, lanes, True, True, every[1:])
+
     def serve_moved(h):
         qc, nq, kc, nk = axes(h)
 
@@ -569,7 +589,7 @@
         if nk == 2:
             each_q(
                 h, lambda j: moved_wanted(h, j) & (j < qc),
-                lambda j: serve(h, j, 1 - kc, lanes, True, True),
+                functools.partial(earlier, h),
             )
             each_q(
                 h, lambda j: moved_wanted(h, j) & (j > qc),
@@ -577,8 +597,48 @@
             )
         else:
             each_q(h, functools.partial(moved_wanted, h), go)
+
+    def spans_of():
+        position = token + me * tok
+        inside = []
+        end = jnp.int32(0)
+        for d in range(docs):
+            begin, end = end, end + lens_ref[d]
+            inside.append((position >= begin) & (position < end))
+        return inside
+
+    def doc_copy(d):
+        return pltpu.make_async_remote_copy(
+            src_ref=docbuf.at[me], dst_ref=docbuf.at[me], send_sem=doc_send.at[d - 1],
+            recv_sem=doc_recv.at[n - d - 1], device_id={"seq": (me + d) % n},
+            device_id_type=MESH,
+        )
+
+    def exchange():
+        for d in range(1, kz):
+            src = (zme + d) % kz
+            pltpu.make_async_remote_copy(
+                src_ref=devbuf.at[src], dst_ref=devbuf.at[src], send_sem=z_send.at[0],
+                recv_sem=z_recv.at[d - 1], device_id={"kvh": src}, device_id_type=MESH,
+            ).wait_recv()
+        deviation = devbuf[0]
+        for z in range(1, kz):
+            deviation = deviation + devbuf[z]
+        dev_ref[...] = deviation
+        inside = spans_of()
+        slot_row = lax.broadcasted_iota(jnp.int32, docbuf.shape[1:], 0)
+        shares = jnp.zeros(docbuf.shape[1:], jnp.float32)
+        for d in range(docs):
+            share = jnp.sum(jnp.where(inside[d], deviation, 0.0), axis=1, keepdims=True)
+            shares = jnp.where(slot_row == d, share, shares)
+        docbuf[me] = shares
+        for d in range(1, n):
+            doc_copy(d).start()
+
+    lens_load.wait()
     for h in range(1, heads, 2):
-        serve_own(h)
+        serve_own(h, True)
+        serve_own(h, False)
     for h in range(heads):
         forward_blocks(h, 0, functools.partial(takes_kv, h))
         if h % 2 == 0:
@@ -587,57 +647,31 @@
             forward_blocks(
                 h, 1, lambda i, h=h: takes_kv(h, i) & jnp.logical_not(shared_link(h, i))
             )
-    for d in range(1, kz):
-        src = (zme + d) % kz
-        pltpu.make_async_remote_copy(
-            src_ref=devbuf.at[src], dst_ref=devbuf.at[src], send_sem=z_send.at[0],
-            recv_sem=z_recv.at[d - 1], device_id={"kvh": src}, device_id_type=MESH,
-        ).wait_recv()
-    lens_load.wait()
-    deviation = devbuf[0]
-    for z in range(1, kz):
-        deviation = deviation + devbuf[z]
-    position = token + me * tok
-    inside = []
-    end = jnp.int32(0)
-    for d in range(docs):
-        begin, end = end, end + lens_ref[d]
-        inside.append((position >= begin) & (position < end))
-    slot_row = lax.broadcasted_iota(jnp.int32, docbuf.shape[1:], 0)
-    shares = jnp.zeros(docbuf.shape[1:], jnp.float32)
-    for d in range(docs):
-        share = jnp.sum(jnp.where(inside[d], deviation, 0.0), axis=1, keepdims=True)
-        shares = jnp.where(slot_row == d, share, shares)
-    docbuf[me] = shares
-    for d in range(1, n):
-        sends.append(
-            pltpu.make_async_remote_copy(
-                src_ref=docbuf.at[me], dst_ref=docbuf.at[me], send_sem=doc_send.at[d - 1],
-                recv_sem=doc_recv.at[n - d - 1], device_id={"seq": (me + d) % n}, device_id_type=MESH,
-            )
-        )
-        sends[-1].start()
     for h in range(1, heads, 2):
         forward_blocks(
             h, 1, lambda i, h=h: takes_kv(h, i) & shared_link(h, i) & (ia < rows_a - 1)
         )
     for h in range(1, heads, 2):
         near_lane(h)
+    pl.when(ia < rows_a - 1)(exchange)
     for h in range(0, heads, 2):
-        serve_own(h, every[:1])
+        serve_own(h, True)
     for h in range(1, heads, 2):
         far_lane(h)
     for h in range(0, heads, 2):
-        serve_own(h, every[1:])
+        serve_own(h, False)
+    last_row = ia == rows_a - 1
+    halved = rows_a == 2 and rows_b == 2 and len(col_parts) > 1
+    corner = last_row & (ib == rows_b - 1) if halved else False
+    pl.when(last_row & jnp.logical_not(corner))(exchange)
     for h in range(0, heads, 2):
         serve_moved(h)
+    for h in range(1, heads, 2):
+        forward_blocks(h, 1, lambda i, h=h: takes_kv(h, i) & (ia == rows_a - 1))
     for h in range(heads):
         qc, nq, kc, nk = axes(h)
         if h % 2 == 1:
-            @pl.when(ia == rows_a - 1)
-            def _():
-                forward_blocks(h, 1, functools.partial(takes_kv, h))
-                arrive(h)
+            pl.when(ia == rows_a - 1)(functools.partial(arrive, h))
         each_k(h, lambda i, kc=kc: i < kc, lambda i, h=h, qc=qc: both(h, qc, i))
     for h in range(heads):
         qc, nq, kc, nk = axes(h)
@@ -671,6 +705,7 @@
             src_ref=docbuf.at[src], dst_ref=docbuf.at[src], send_sem=doc_send.at[0],
             recv_sem=doc_recv.at[d - 1], device_id={"seq": src}, device_id_type=MESH,
         ).wait_recv()
+    inside = spans_of()
     totals = docbuf[0]
     for s in range(1, n):
         totals = totals + docbuf[s]
@@ -678,9 +713,11 @@
     for d in range(docs):
         here = totals[d:d + 1, 0:1] / lens_ref[d].astype(jnp.float32)
         mean = jnp.where(inside[d], here, mean)
-    score_ref[...] = deviation / (mean + 1.0)
+    score_ref[...] = dev_ref[...] / (mean + 1.0)
     for send in sends:
         send.wait_send()
+    for d in range(1, n):
+        doc_copy(d).wait_send()
     for h in range(heads):
         qc, nq, kc, nk = axes(h)
 
@@ -761,6 +798,7 @@
             pltpu.VMEM((tok, pad), f32),
             pltpu.VMEM((tok, LANES), f32),
             pltpu.VMEM((tok - cut, tok), bf),
+            pltpu.VMEM((1, tok), f32),
             pltpu.VMEM((kz, 1, tok), f32),
             pltpu.VMEM((n, round_up(docs, 8), 128), f32),
             pltpu.SMEM(doc_lengths.shape, jnp.int32),

time: 24.6 us -> 24.5 us (level)
  no operation moved by 1% of the time
where the time goes in v6:
time: 24.5 us; the launch traced here: 24.3 us
  Pallas kernels  22.4 us (91%)
  local copies, waits for them, and re-layouts  0.7 us (3%)
  between operations  0.64 us (3%)
  other arithmetic  0.6 us (2%)
    pallas_call x1, Pallas kernels, shards(): pl.pallas_call(functools.partial(kernel, n, kz, docs, sel_rows), out_shap...  22.4 us
    unnamed x1, local copies, waits for them, and re-layouts  0.7 us
    pallas_call x1, other arithmetic, shards(): pl.pallas_call(functools.partial(kernel, n, kz, docs, sel_rows), out_shap...  0.6 us

profile of v6, /device:TPU:0, one launch (start us, length us, event | category | flops | bytes accessed | tf_op | source)
XLA Modules:
  0.0 24.3 jit_solution(17551045551079179561)
XLA Ops:
  0.6 22.4 %blend.1 = (bf16[120,1024]{1,0:T(8,128)(2,1)S(1)}, f32[1,768]{1,0:T(1,128)S(1)}) custom-call(bf16[768,4096]{1,0:T(8,128)(2,1)} %hid_hbm.1, bf16[4096,1024]{1,0:T(8,128)(2,1)} %wq_hbm.1, bf16[4096,256]{1,0:T(8,128)(2,1)} %wk_hbm.1, bf16[4096,256]{1,0:T(8,128)(2,1)} %wv_hbm.1, bf16[768,256]{1,0:T(8,128)(2,1)} %ck_hbm.1, bf16[768,256]{1,0:T(8,128)(2,1)} %cv_hbm.1, ...), custom_call_target="tpu_custom_call" | custom-call | tf_op jit(solution)/shard_map/blend/pallas_call | solution.py:769
  23.0 0.7 %copy.11 = bf16[120,1024]{1,0:T(8,128)(2,1)} copy(bf16[120,1024]{1,0:T(8,128)(2,1)S(1)} %get-tuple-element.6) | data formatting | bytes 491520
  23.7 0.6 %reduce = f32[768]{0:T(1024)} reduce(f32[1,768]{1,0:T(1,128)S(1)} %get-tuple-element.5, f32[]{:T(128)} %constant), dimensions={0}, to_apply=%get-tuple-element.5.reduce_sub_computation | reduce | bytes 6148 | tf_op jit(solution)/shard_map/blend/pallas_call | solution.py:769

commit v7 on v6

--- a/solution.py
+++ b/solution.py
@@ -568,9 +568,10 @@
 
     def earlier(h, j):
         other = 1 - axes(h)[2]
-        serve(h, j, other, lanes, True, True, every[:1])
+        serve(h, j, other, lanes, True, False, every[:1])
         if h == 0 and halved:
             pl.when(corner)(exchange)
+        give_back(h, j, 0)
         serve(h, j, other, lanes, True, True, every[1:])
 
     def serve_moved(h):

time: 24.5 us -> 24.5 us (level)
  no operation moved by 1% of the time
where the time goes in v7:
time: 24.5 us; the launch traced here: 24.3 us
  Pallas kernels  22.4 us (91%)
  local copies, waits for them, and re-layouts  0.7 us (3%)
  between operations  0.64 us (3%)
  other arithmetic  0.6 us (2%)
    pallas_call x1, Pallas kernels, shards(): pl.pallas_call(functools.partial(kernel, n, kz, docs, sel_rows), out_shap...  22.4 us
    unnamed x1, local copies, waits for them, and re-layouts  0.7 us
    pallas_call x1, other arithmetic, shards(): pl.pallas_call(functools.partial(kernel, n, kz, docs, sel_rows), out_shap...  0.6 us

profile of v7, /device:TPU:0, one launch (start us, length us, event | category | flops | bytes accessed | tf_op | source)
XLA Modules:
  0.0 24.3 jit_solution(8952321028420838722)
XLA Ops:
  0.6 22.4 %blend.1 = (bf16[120,1024]{1,0:T(8,128)(2,1)S(1)}, f32[1,768]{1,0:T(1,128)S(1)}) custom-call(bf16[768,4096]{1,0:T(8,128)(2,1)} %hid_hbm.1, bf16[4096,1024]{1,0:T(8,128)(2,1)} %wq_hbm.1, bf16[4096,256]{1,0:T(8,128)(2,1)} %wk_hbm.1, bf16[4096,256]{1,0:T(8,128)(2,1)} %wv_hbm.1, bf16[768,256]{1,0:T(8,128)(2,1)} %ck_hbm.1, bf16[768,256]{1,0:T(8,128)(2,1)} %cv_hbm.1, ...), custom_call_target="tpu_custom_call" | custom-call | tf_op jit(solution)/shard_map/blend/pallas_call | solution.py:770
  23.0 0.7 %copy.11 = bf16[120,1024]{1,0:T(8,128)(2,1)} copy(bf16[120,1024]{1,0:T(8,128)(2,1)S(1)} %get-tuple-element.6) | data formatting | bytes 491520
  23.7 0.6 %reduce = f32[768]{0:T(1024)} reduce(f32[1,768]{1,0:T(1,128)S(1)} %get-tuple-element.5, f32[]{:T(128)} %constant), dimensions={0}, to_apply=%get-tuple-element.5.reduce_sub_computation | reduce | bytes 6148 | tf_op jit(solution)/shard_map/blend/pallas_call | solution.py:770
